TPU v7x, 32 devices: a whole 2x2x4 slice. The times are simulated.
32 devices in a mesh: dp: 8 (over y, x, core), expert: 4 (over z).
Axes of the slice: x: 2, y: 2, z: 4, core: 2. Of those that a mesh axis runs over, the one named last changes fastest.
Arguments:
- tokens: bfloat16 [512, 4096], P('expert', 'dp'), may hold values from -6 to 6
- in_signs: int32 [512, 128], P('expert', 'dp'), may hold values from -2147483648 to 2147483646
- out_signs: int32 [512, 224], P('expert'), may hold values from -2147483648 to 2147483646
- expert_ids: int32 [512, 2], P('expert'), may hold values from 0 to 3, all different within a row; in each aligned block of 128 rows (0 to 127, 128 to 255, ...) at most 80 rows name the same one
- route_weight: float32 [512, 2], P('expert'), may hold values from 0.2 to 1
- cotangent: bfloat16 [512, 7168], P('expert', 'dp'), may hold values from -6 to 6
- mean_weight: bfloat16 [4, 4096, 7168], P('expert', 'dp'), may hold values from -0.09375 to 0.09375
- rho_weight: bfloat16 [4, 4096, 7168], P('expert', 'dp'), may hold values from -6 to -3
- noise_weight: bfloat16 [4, 4096, 7168], P('expert', 'dp'), may hold values from -4 to 4
Outputs:
- hidden_out: bfloat16 [512, 7168], P('expert', 'dp')
- grad_tokens: bfloat16 [512, 4096], P('expert', 'dp')
- grad_mean: bfloat16 [4, 4096, 7168], P('expert', 'dp')
- grad_rho: bfloat16 [4, 4096, 7168], P('expert', 'dp')
Inputs may be any that keep to these rules, and one draw needn't show every extreme that they name: `expert_ids`: each token names 2 different experts. In each aligned block of 128 tokens no expert is named by more than 80 tokens, and in some blocks one expert is named by exactly 80. `in_signs`: bit b of word w, counted from the lowest, is set where the sign of feature 32 * w + b is -1 and clear where it is +1. `out_signs`: bit b of word w, counted from the lowest, is set where the sign of hidden unit 32 * w + b is -1 and clear where it is +1.
All inputs are finite; a program needn't handle non-finite values.
Results may differ from a plain program's by a relative error of at most 0.0071.
Values may be sent and summed in bfloat16 or wider, within the bound.
A program may use at most 128 MiB of HBM per device.

v0:
```python
import functools

import jax
import jax.numpy as jnp
from jax import lax
from jax.experimental import pallas as pl
from jax.experimental.pallas import tpu as pltpu
from jax.sharding import PartitionSpec as P

def unpack_rows(words):
    shifts = jnp.arange(32, dtype=jnp.int32)
    bits = jnp.bitwise_and(jnp.right_shift(words[..., None], shifts), 1)
    signs = (1 - 2 * bits).astype(jnp.float32)
    return signs.reshape(words.shape[:-1] + (words.shape[-1] * 32,))


def unpack_cols(words):
    shifts = jnp.arange(32, dtype=jnp.int32)
    bits = jnp.bitwise_and(jnp.right_shift(words.T[:, None, :], shifts[None, :, None]), 1)
    signs = (1 - 2 * bits).astype(jnp.float32)
    return signs.reshape(words.shape[1] * 32, words.shape[0])


def block_slots(block_ids, experts, capacity):
    onehot = (block_ids[:, :, None] == jnp.arange(experts, dtype=jnp.int32)).astype(jnp.int32)
    flat = onehot.reshape(-1, experts)
    before = jnp.cumsum(flat, axis=0) - flat
    ranks = jnp.sum(before * flat, axis=1).reshape(block_ids.shape)
    return block_ids * capacity + ranks


def on_device_general(
    tokens,
    in_signs,
    out_signs,
    expert_ids,
    route_weight,
    cotangent,
    mean_weight,
    rho_weight,
    noise_weight,
):
    experts = lax.axis_size("expert") * mean_weight.shape[0]
    token_count = tokens.shape[0]
    topk = expert_ids.shape[1]
    capacity = 5 * token_count * topk // (4 * experts)
    slots = experts * capacity
    width_local = tokens.shape[1]
    sign_words = in_signs.shape[1]
    hidden_local = cotangent.shape[1]
    slot_of = block_slots(expert_ids, experts, capacity)
    match = (slot_of[:, :, None] == jnp.arange(slots, dtype=jnp.int32)).astype(jnp.int32)
    token_rank = jnp.arange(token_count, dtype=jnp.int32)[:, None, None]
    slot_token = jnp.sum(match * token_rank, axis=(0, 1))
    slot_fill = jnp.sum(match, axis=(0, 1))
    slot_weight = jnp.sum(match.astype(jnp.float32) * route_weight[:, :, None], axis=(0, 1))
    words = jnp.concatenate([in_signs, out_signs], axis=1)
    fill_rows = slot_fill.astype(jnp.bfloat16)[:, None]
    send_rows = (jnp.take(tokens, slot_token, axis=0) * fill_rows).reshape(
        experts, capacity, width_local
    )
    send_words = jnp.take(words, slot_token, axis=0).reshape(experts, capacity, words.shape[1])
    recv_rows, recv_words = (
        lax.all_to_all(send_rows, "expert", split_axis=0, concat_axis=0, tiled=True),
        lax.all_to_all(send_words, "expert", split_axis=0, concat_axis=0, tiled=True),
    )
    rows = recv_rows.reshape(slots, width_local)
    recv_words = recv_words.reshape(slots, words.shape[1])
    input_signs = unpack_rows(recv_words[:, :sign_words])
    input_cols = unpack_cols(recv_words[:, :sign_words])
    signed = rows * input_signs.astype(jnp.bfloat16)
    mean_local = mean_weight[0]
    rho_float = rho_weight[0].astype(jnp.float32)
    noise_float = noise_weight[0].astype(jnp.float32)
    delta = (jax.nn.softplus(rho_float) * noise_float).astype(jnp.bfloat16)
    contract = (((0,), (1,)), ((), ()))
    output_cols = unpack_cols(recv_words[:, sign_words:])
    mean_cols = mean_local
    delta_cols = delta
    mean_part = lax.dot_general(mean_cols, rows, contract, preferred_element_type=jnp.float32)
    pert_part = lax.dot_general(delta_cols, signed, contract, preferred_element_type=jnp.float32)
    mean_part, pert_part = (mean_part, pert_part)
    preact = lax.psum_scatter(
        mean_part + output_cols * pert_part, "dp", scatter_dimension=0, tiled=True
    )
    gate = jax.nn.sigmoid(preact)
    hidden_slots = (preact * gate).astype(jnp.bfloat16)
    slope = gate * (1.0 + preact * (1.0 - gate))
    returned = lax.all_to_all(
        hidden_slots.reshape(hidden_local, experts, capacity),
        "expert",
        split_axis=1,
        concat_axis=1,
        tiled=True,
    )
    returned = returned.reshape(hidden_local, slots)
    picked = jnp.take(returned, slot_of, axis=1).astype(jnp.float32)
    hidden_out = jnp.sum(picked * route_weight[None], axis=2).T.astype(jnp.bfloat16)
    upstream = jnp.take(cotangent.T, slot_token, axis=1).astype(jnp.float32) * slot_weight[None, :]
    upstream = upstream.astype(jnp.bfloat16).reshape(hidden_local, experts, capacity)
    arrived = lax.all_to_all(upstream, "expert", split_axis=1, concat_axis=1, tiled=True).reshape(
        hidden_local, slots
    )
    grad_preact = (arrived.astype(jnp.float32) * slope).astype(jnp.bfloat16)
    piece = lax.all_gather(grad_preact, "dp", axis=0, tiled=True)
    piece_signed = piece * output_cols.astype(jnp.bfloat16)
    mean_cols = mean_local
    delta_cols = delta
    grad_rows = jnp.dot(mean_cols, piece, preferred_element_type=jnp.float32)
    grad_signed = jnp.dot(delta_cols, piece_signed, preferred_element_type=jnp.float32)
    mean_block = lax.dot_general(rows, piece, contract, preferred_element_type=jnp.float32)
    delta_block = lax.dot_general(
        signed, piece_signed, contract, preferred_element_type=jnp.float32
    )
    grad_mean_acc = mean_block
    grad_delta_acc = delta_block
    result = (grad_rows, grad_signed, grad_mean_acc, grad_delta_acc)
    grad_rows, grad_signed, grad_mean_acc, grad_delta_acc = result
    slot_grad = (grad_rows + input_cols * grad_signed).astype(jnp.bfloat16)
    back = lax.all_to_all(
        slot_grad.reshape(width_local, experts, capacity),
        "expert",
        split_axis=1,
        concat_axis=1,
        tiled=True,
    )
    back = back.reshape(width_local, slots)
    grad_tokens = jnp.sum(jnp.take(back, slot_of, axis=1).astype(jnp.float32), axis=2).T.astype(
        jnp.bfloat16
    )
    grad_mean = grad_mean_acc.astype(jnp.bfloat16)[None]
    grad_rho = (grad_delta_acc * noise_float * jax.nn.sigmoid(rho_float)).astype(jnp.bfloat16)[None]
    return (hidden_out, grad_tokens, grad_mean, grad_rho)


LANES = 128
VMEM_LIMIT = 56 * 1024 * 1024


def cost(flops, nbytes, trans=0):
    return pl.CostEstimate(flops=flops, bytes_accessed=nbytes, transcendentals=trans)


def params():
    return pltpu.CompilerParams(
        dimension_semantics=("arbitrary",), vmem_limit_bytes=VMEM_LIMIT
    )


def lane_signs(words, first, tiles):
    slots, total = words.shape
    lane = lax.broadcasted_iota(jnp.int32, (slots, LANES), 1)
    shift = lane % 32
    out = []
    for tile in range(tiles):
        at = first + 4 * tile + lane // 32
        picked = None
        for part in range(total // LANES):
            piece = jnp.take_along_axis(
                words[:, part * LANES : (part + 1) * LANES],
                at % LANES,
                axis=1,
                mode="promise_in_bounds",
            )
            picked = piece if part == 0 else jnp.where(at >= part * LANES, piece, picked)
        bits = jnp.bitwise_and(jnp.right_shift(picked, shift), 1)
        out.append((1 - 2 * bits).astype(jnp.float32))
    return jnp.concatenate(out, axis=1) if tiles > 1 else out[0]


def delta_kernel(rho_ref, noise_ref, delta_ref):
    rho = rho_ref[...].astype(jnp.float32)
    noise = noise_ref[...].astype(jnp.float32)
    soft = jnp.maximum(rho, 0.0) + jnp.log(1.0 + jnp.exp(-jnp.abs(rho)))
    delta_ref[...] = (soft * noise).astype(delta_ref.dtype)


def make_delta(rho, noise, rows=64):
    width, hidden = rho.shape
    spec = pl.BlockSpec((rows, hidden), lambda i: (i, 0))
    return pl.pallas_call(
        delta_kernel,
        grid=(width // rows,),
        in_specs=[spec, spec],
        out_specs=spec,
        out_shape=jax.ShapeDtypeStruct((width, hidden), jnp.bfloat16),
        compiler_params=params(),
        cost_estimate=cost(20 * width * hidden, 6 * width * hidden, 2 * width * hidden),
        name="delta",
    )(rho, noise)


def forward_kernel(in_words, words_ref, rows_ref, mean_ref, delta_ref, y_ref, r_ref, b_ref, s_ref):
    step = pl.program_id(0)
    block = mean_ref.shape[1]
    words = words_ref[...]

    @pl.when(step == 0)
    def _():
        signs = lane_signs(words, 0, rows_ref.shape[1] // LANES).astype(jnp.bfloat16)
        s_ref[...] = signs
        b_ref[...] = rows_ref[...] * signs

    signs = lane_signs(words, in_words + step * (block // 32), block // LANES)
    r_ref[0] = signs.astype(jnp.bfloat16)
    mean_part = jnp.dot(rows_ref[...], mean_ref[...], preferred_element_type=jnp.float32)
    pert_part = jnp.dot(b_ref[...], delta_ref[...], preferred_element_type=jnp.float32)
    y_ref[0] = (mean_part + signs * pert_part).astype(y_ref.dtype)


def forward(words, rows, mean, delta, parts, in_words):
    slots, width = rows.shape
    hidden = mean.shape[1]
    block = hidden // parts
    whole = lambda shape: pl.BlockSpec(shape, lambda i: (0, 0))
    weight = pl.BlockSpec((width, block), lambda i: (0, i))
    piece = pl.BlockSpec((1, slots, block), lambda i: (i, 0, 0))
    small = jax.ShapeDtypeStruct((slots, width), jnp.bfloat16)
    large = jax.ShapeDtypeStruct((parts, slots, block), jnp.bfloat16)
    return pl.pallas_call(
        functools.partial(forward_kernel, in_words),
        grid=(parts,),
        in_specs=[whole(words.shape), whole(rows.shape), weight, weight],
        out_specs=[piece, piece, whole(rows.shape), whole(rows.shape)],
        out_shape=[large, large, small, small],
        compiler_params=params(),
        cost_estimate=cost(4 * slots * width * hidden, 4 * hidden * (width + slots)),
        name="forward",
    )(words, rows, mean, delta)


NT = (((1,), (1,)), ((), ()))


def back_kernel(dy_ref, r_ref, mean_ref, delta_ref, s_ref, g_ref, plain, signed):
    step = pl.program_id(0)
    dy = dy_ref[0]
    one = lax.dot_general(dy, mean_ref[...], NT, preferred_element_type=jnp.float32)
    two = lax.dot_general(dy * r_ref[0], delta_ref[...], NT, preferred_element_type=jnp.float32)

    @pl.when(step == 0)
    def _():
        plain[...] = one
        signed[...] = two

    @pl.when(step > 0)
    def _():
        plain[...] += one
        signed[...] += two

    @pl.when(step == pl.num_programs(0) - 1)
    def _():
        total = plain[...] + s_ref[...].astype(jnp.float32) * signed[...]
        g_ref[...] = total.astype(g_ref.dtype)


def back(dy, r, mean, delta, s):
    parts, slots, block = dy.shape
    width = mean.shape[0]
    hidden = parts * block
    weight = pl.BlockSpec((width, block), lambda i: (0, i))
    piece = pl.BlockSpec((1, slots, block), lambda i: (i, 0, 0))
    whole = pl.BlockSpec((slots, width), lambda i: (0, 0))
    return pl.pallas_call(
        back_kernel,
        grid=(parts,),
        in_specs=[piece, piece, weight, weight, whole],
        out_specs=whole,
        out_shape=jax.ShapeDtypeStruct((slots, width), jnp.bfloat16),
        scratch_shapes=[pltpu.VMEM((slots, width), jnp.float32)] * 2,
        compiler_params=params(),
        cost_estimate=cost(4 * slots * width * hidden, 4 * hidden * (width + slots)),
        name="back",
    )(dy, r, mean, delta, s)


def grads_kernel(dy_ref, r_ref, rho_ref, noise_ref, at_ref, bt_ref, gm_ref, gr_ref):
    dy = dy_ref[0]
    gm = jnp.dot(at_ref[...], dy, preferred_element_type=jnp.float32)
    gm_ref[...] = gm.astype(gm_ref.dtype)
    gd = jnp.dot(bt_ref[...], dy * r_ref[0], preferred_element_type=jnp.float32)
    gate = 1.0 / (1.0 + jnp.exp(-rho_ref[...].astype(jnp.float32)))
    gr_ref[...] = (gd * noise_ref[...].astype(jnp.float32) * gate).astype(gr_ref.dtype)


def grads(dy, r, rho, noise, at, bt):
    parts, slots, block = dy.shape
    width, hidden = rho.shape
    weight = pl.BlockSpec((width, block), lambda i: (0, i))
    piece = pl.BlockSpec((1, slots, block), lambda i: (i, 0, 0))
    whole = pl.BlockSpec((width, slots), lambda i: (0, 0))
    out = jax.ShapeDtypeStruct((width, hidden), jnp.bfloat16)
    return pl.pallas_call(
        grads_kernel,
        grid=(parts,),
        in_specs=[piece, piece, weight, weight, whole, whole],
        out_specs=[weight, weight],
        out_shape=[out, out],
        compiler_params=params(),
        cost_estimate=cost(4 * slots * width * hidden, 8 * hidden * (width + slots)),
        name="grads",
    )(dy, r, rho, noise, at, bt)


def exchange_kernel(
    p_ref, up_ref, out_ref, back_ref, arr, rd, cs, ra, rb, rc, h_ref, send_sem, recv_sem
):
    me = lax.axis_index("dp")
    mine = lax.axis_index("expert")
    ranks = up_ref.shape[0]
    cap = up_ref.shape[1]
    half = p_ref.shape[1] // 2
    y, x, c = me // 4, (me // 2) % 2, me % 2
    place = lambda dy, dx, dc: ((y + dy) % 2) * 4 + ((x + dx) % 2) * 2 + (c + dc) % 2
    at_x, at_y, at_c = place(0, 1, 0), place(1, 0, 0), place(0, 0, 1)
    rows = [pl.ds(0, half), pl.ds(half, half)]
    peers = [(at_x, mine), (at_y, mine), (at_c, mine)]
    peers += [(me, (mine + j) % ranks) for j in range(1, ranks)]
    count = [0]
    started = []

    def send(src, dst, to):
        n = count[0]
        count[0] += 1
        copy = pltpu.make_async_remote_copy(
            src_ref=src,
            dst_ref=dst,
            send_sem=send_sem.at[n],
            recv_sem=recv_sem.at[n],
            device_id=to,
            device_id_type=pl.DeviceIdType.MESH,
        )
        copy.start()
        started.append(copy)
        return copy

    barrier = pltpu.get_barrier_semaphore()
    for peer in peers:
        pl.semaphore_signal(barrier, inc=1, device_id=peer, device_id_type=pl.DeviceIdType.MESH)
    pl.semaphore_wait(barrier, len(peers))

    order = (3, 1, 2, 0)
    core = {
        k: send(p_ref.at[place(k // 2, k % 2, 1)], rd.at[k], (at_c, mine)) for k in order
    }
    to_owner = [
        send(up_ref.at[(mine + j) % ranks], arr.at[mine], (me, (mine + j) % ranks))
        for j in range(1, ranks)
    ]
    arr[mine] = up_ref[mine]

    def add(*terms):
        total = terms[0].astype(jnp.float32)
        for term in terms[1:]:
            total = total + term.astype(jnp.float32)
        return total

    def chip_sum(k, which):
        at = rows[which]
        cs[k, at] = add(p_ref[place(k // 2, k % 2, 0), at], rd[k, at]).astype(cs.dtype)

    core[3].wait_recv()
    chip_sum(3, 0)
    along_x = [send(cs.at[3, rows[0]], ra.at[1], (at_x, mine))]
    chip_sum(3, 1)
    along_y = [send(cs.at[3, rows[1]], rb.at[1], (at_y, mine))]
    core[1].wait_recv()
    chip_sum(1, 0)
    along_x.append(send(cs.at[1, rows[0]], ra.at[0], (at_x, mine)))
    core[2].wait_recv()
    chip_sum(2, 1)
    along_y.append(send(cs.at[2, rows[1]], rb.at[0], (at_y, mine)))
    along_x[0].wait_recv()
    at = rows[0]
    cs[2, at] = add(p_ref[place(1, 0, 0), at], rd[2, at], ra[1]).astype(cs.dtype)
    last_y = send(cs.at[2, at], rc.at[0], (at_y, mine))
    along_y[0].wait_recv()
    at = rows[1]
    cs[1, at] = add(p_ref[place(0, 1, 0), at], rd[1, at], rb[1]).astype(cs.dtype)
    last_x = send(cs.at[1, at], rc.at[1], (at_x, mine))
    core[0].wait_recv()
    for copy in to_owner:
        copy.wait_recv()

    def activate(which, near):
        per = ranks // 2
        for i in range(per):
            own = pl.ds(which * half + i * cap, cap)
            part = pl.ds(i * cap, cap)
            preact = add(p_ref[me, own], rd[0, own], near[0, part], rc[which, part])
            gate = 1.0 / (1.0 + jnp.exp(-preact))
            h_ref[which * per + i] = (preact * gate).astype(h_ref.dtype)
            slope = gate * (1.0 + preact * (1.0 - gate))
            up = arr[which * per + i].astype(jnp.float32)
            out_ref[me, own] = (up * slope).astype(out_ref.dtype)

    def spread(owner, which, to):
        piece = out_ref.at[owner, rows[which]]
        return send(piece, piece, (to, mine))

    along_x[1].wait_recv()
    last_y.wait_recv()
    activate(0, ra)
    y_one = spread(me, 0, at_y)
    x_two = spread(me, 0, at_x)
    c_all = [spread(me, 0, at_c)]
    along_y[1].wait_recv()
    last_x.wait_recv()
    activate(1, rb)
    x_one = spread(me, 1, at_x)
    y_two = spread(me, 1, at_y)
    c_all.append(spread(me, 1, at_c))
    to_token = [
        send(h_ref.at[(mine + j) % ranks], back_ref.at[mine], (me, (mine + j) % ranks))
        for j in range(1, ranks)
    ]
    back_ref[mine] = h_ref[mine]
    y_one.wait_recv()
    x_three = spread(at_y, 0, at_x)
    c_all.append(spread(at_y, 0, at_c))
    x_one.wait_recv()
    y_three = spread(at_x, 1, at_y)
    c_all.append(spread(at_x, 1, at_c))
    x_two.wait_recv()
    c_all.append(spread(at_x, 0, at_c))
    y_two.wait_recv()
    c_all.append(spread(at_y, 1, at_c))
    x_three.wait_recv()
    c_all.append(spread(place(1, 1, 0), 0, at_c))
    y_three.wait_recv()
    c_all.append(spread(place(1, 1, 0), 1, at_c))
    for copy in c_all + to_token:
        copy.wait_recv()
    for copy in started:
        copy.wait_send()


def exchange(partial, upstream):
    parts, slots, block = partial.shape
    ranks, cap, _ = upstream.shape
    bf16 = jnp.bfloat16
    vmem = pl.BlockSpec(memory_space=pltpu.VMEM)
    copies = 4 + 4 + 2 + 6 + 8 + 2 * (ranks - 1)
    half = (2, slots // 2, block)
    return pl.pallas_call(
        exchange_kernel,
        in_specs=[vmem, vmem],
        out_specs=[vmem, vmem],
        out_shape=[
            jax.ShapeDtypeStruct(partial.shape, bf16),
            jax.ShapeDtypeStruct(upstream.shape, bf16),
        ],
        scratch_shapes=[
            pltpu.VMEM(upstream.shape, bf16),
            pltpu.VMEM((4, slots, block), bf16),
            pltpu.VMEM((4, slots, block), bf16),
            pltpu.VMEM(half, bf16),
            pltpu.VMEM(half, bf16),
            pltpu.VMEM(half, bf16),
            pltpu.VMEM(upstream.shape, bf16),
            pltpu.SemaphoreType.DMA((copies,)),
            pltpu.SemaphoreType.DMA((copies,)),
        ],
        compiler_params=pltpu.CompilerParams(
            collective_id=0, has_side_effects=True, vmem_limit_bytes=VMEM_LIMIT
        ),
        cost_estimate=cost(10 * partial.size, 100 * partial.size),
        name="exchange",
    )(partial, upstream)


def exact_dot(onehot, values):
    return jnp.dot(onehot, values, preferred_element_type=jnp.float32)


def on_device(
    tokens,
    in_signs,
    out_signs,
    expert_ids,
    route_weight,
    cotangent,
    mean_weight,
    rho_weight,
    noise_weight,
):
    parts = lax.axis_size("dp")
    token_count = tokens.shape[0]
    hidden_local = cotangent.shape[1]
    width_local = tokens.shape[1]
    ranks = lax.axis_size("expert")
    fits = parts == 8 and ranks % 2 == 0 and mean_weight.shape[0] == 1
    if not fits or hidden_local % LANES or width_local % LANES or token_count % 128:
        return on_device_general(
            tokens,
            in_signs,
            out_signs,
            expert_ids,
            route_weight,
            cotangent,
            mean_weight,
            rho_weight,
            noise_weight,
        )
    experts = ranks
    topk = expert_ids.shape[1]
    capacity = 5 * token_count * topk // (4 * experts)
    slots = experts * capacity
    in_words = in_signs.shape[1]
    mean, rho, noise = mean_weight[0], rho_weight[0], noise_weight[0]
    slot_of = block_slots(expert_ids, experts, capacity)
    match = slot_of[:, :, None] == jnp.arange(slots, dtype=jnp.int32)
    take_of = [match[:, k, :].astype(jnp.bfloat16) for k in range(topk)]
    fill_of = jnp.sum(match.astype(jnp.float32), axis=1).astype(jnp.bfloat16)
    slot_weight = jnp.sum(match.astype(jnp.float32) * route_weight[:, :, None], axis=(0, 1))
    token_rank = jnp.arange(token_count, dtype=jnp.int32)[:, None, None]
    slot_token = jnp.sum(match.astype(jnp.int32) * token_rank, axis=(0, 1))
    words = jnp.concatenate([in_signs, out_signs], axis=1)
    words = jnp.pad(words, ((0, 0), (0, -words.shape[1] % LANES)))
    send_words = jnp.take(words, slot_token, axis=0).reshape(experts, capacity, -1)
    fill_t = fill_of.T
    send_rows = exact_dot(fill_t, tokens).astype(jnp.bfloat16)
    upstream = (exact_dot(fill_t, cotangent) * slot_weight[:, None]).astype(jnp.bfloat16)
    swap = functools.partial(
        lax.all_to_all, axis_name="expert", split_axis=0, concat_axis=0, tiled=True
    )
    recv_rows = swap(send_rows.reshape(experts, capacity, -1)).reshape(slots, -1)
    recv_words = swap(send_words).reshape(slots, -1)
    delta = make_delta(rho, noise)
    partial, r, signed, s = forward(recv_words, recv_rows, mean, delta, parts, in_words)
    dy_all, returned = exchange(partial, upstream.reshape(experts, capacity, -1))
    returned = returned.reshape(slots, -1)
    hidden_out = sum(
        exact_dot(take_of[k], returned) * route_weight[:, k][:, None] for k in range(topk)
    ).astype(jnp.bfloat16)
    g = back(dy_all, r, mean, delta, s)
    g_back = swap(g.reshape(experts, capacity, -1)).reshape(slots, -1)
    grad_mean, grad_rho = grads(dy_all, r, rho, noise, recv_rows.T, signed.T)
    grad_tokens = exact_dot(fill_of, g_back).astype(jnp.bfloat16)
    return (hidden_out, grad_tokens, grad_mean[None], grad_rho[None])


def solution(mesh):
    in_specs = (
        P("expert", "dp"),
        P("expert", "dp"),
        P("expert", None),
        P("expert", None),
        P("expert", None),
        P("expert", "dp"),
        P("expert", "dp", None),
        P("expert", "dp", None),
        P("expert", "dp", None),
    )
    out_specs = (
        P("expert", "dp"),
        P("expert", "dp"),
        P("expert", "dp", None),
        P("expert", "dp", None),
    )
    return jax.shard_map(
        on_device, mesh=mesh, in_specs=in_specs, out_specs=out_specs, check_vma=False
    )
```

profile of v0, /device:TPU:0, one launch (start us, length us, event | category | flops | bytes accessed | tf_op | source)
XLA Modules:
  0.0 151.5 jit_solution(3878893395476031426)
XLA Ops:
  0.6 0.0 copy-start
  0.6 0.8 copy.44
  1.5 0.1 eq.43
  1.6 0.1 eq.39
  1.8 1.2 reduce-window.6
  3.0 0.1 slice.26
  3.1 0.1 copy.46
  3.2 0.1 copy.47
  3.3 0.1 add_bitcast_fusion
  3.4 0.1 reshape.75
  3.6 0.1 copy.48
  3.6 0.7 multiply_add_fusion
  4.3 0.1 select_reduce_fusion.1
  4.5 0.8 copy.49
  5.3 1.0 copy.50
  6.3 0.1 pad_add_fusion
  6.4 1.6 %gather_fusion = s32[320,240]{1,0:T(8,128)S(1)} fusion(s32[128,240]{1,0:T(8,128)S(1)} %pad_add_fusion, s32[1024]{0:T(1024)S(1)} %pad_clamp_fusion), kind=kCustom, calls=%fused_computation | custom fusion | bytes 615680 | tf_op jit(solution)/shard_map/jit(_take)/gather | solution.py:520
  8.1 0.8 pad_select_fusion
  8.9 6.3 %all-to-all-start = ((s32[4,80,256]{2,1,0:T(8,128)}), s32[4,80,256]{2,1,0:T(8,128)S(1)}, u32[]{:S(2)}, u32[]{:S(2)}) async-start(s32[4,80,256]{2,1,0:T(8,128)} %bitcast.3), calls=%async_computation | async-start | bytes 655360 | tf_op jit(solution)/shard_map/all_to_all | solution.py:528
  15.2 0.8 select_reduce_fusion
  16.1 1.9 %convolution_convert_fusion = bf16[320,512]{1,0:T(8,128)(2,1)} fusion(bf16[128,512]{1,0:T(8,128)(2,1)} %param.9, bf16[128,320]{0,1:T(8,128)(2,1)S(1)} %get-tuple-element.21), kind=kOutput, calls=%fused_computation.3 | convolution fusion | flops 42106880 | bytes 540672 | tf_op jit(solution)/shard_map/dot_general | solution.py:473
  17.9 7.6 %all-to-all-done = s32[4,80,256]{2,1,0:T(8,128)S(1)} async-done(((s32[4,80,256]{2,1,0:T(8,128)}), s32[4,80,256]{2,1,0:T(8,128)S(1)}, u32[]{:S(2)}, u32[]{:S(2)}) %all-to-all-start) | async-done | bytes 327712 | tf_op jit(solution)/shard_map/all_to_all | solution.py:528
  25.6 3.5 %all-to-all-start.1 = ((bf16[4,80,512]{2,1,0:T(8,128)(2,1)}), bf16[4,80,512]{2,1,0:T(8,128)(2,1)S(1)}, u32[]{:S(2)}, u32[]{:S(2)}) async-start(bf16[4,80,512]{2,1,0:T(8,128)(2,1)} %bitcast.5), calls=%async_computation.1 | async-start | bytes 655360 | tf_op jit(solution)/shard_map/all_to_all | solution.py:527
  29.0 0.8 slice_bitcast_fusion.4
  29.8 12.4 %delta.1.delta_ref = bf16[512,7168]{1,0:T(8,128)(2,1)} custom-call(bf16[512,7168]{1,0:T(8,128)(2,1)} %bitcast.52, bf16[512,7168]{1,0:T(8,128)(2,1)} %bitcast.54), custom_call_target="tpu_custom_call" | custom-call | flops 73400320 | bytes 22020096 | tf_op jit(solution)/shard_map/delta/pallas_call | solution.py:181
  42.2 0.0 copy-done.4
  42.2 0.1 iota_compare_fusion
  42.2 0.0 copy-done
  42.2 1.1 fusion
  43.3 0.0 all-to-all-done.1
  43.4 0.7 copy-done.2
  44.1 13.5 %forward.1 = (bf16[8,320,896]{2,1,0:T(8,128)(2,1)}, bf16[8,320,896]{2,1,0:T(8,128)(2,1)}, bf16[320,512]{1,0:T(8,128)(2,1)}, bf16[320,512]{1,0:T(8,128)(2,1)}) custom-call(s32[320,256]{1,0:T(8,128)} %bitcast.67, bf16[320,512]{1,0:T(8,128)(2,1)} %bitcast.63, bf16[512,7168]{1,0:T(8,128)(2,1)} %bitcast.56, bf16[512,7168]{1,0:T(8,128)(2,1)} %delta.1.delta_ref), custom_call_target="tpu_custom_call" | custom-call | flops 4697620480 | bytes 23855104 | tf_op jit(solution)/shard_map/forward/pallas_call | solution.py:220
  57.6 53.9 %exchange.1 = (bf16[8,320,896]{2,1,0:T(8,128)(2,1)}, bf16[4,80,896]{2,1,0:T(8,128)(2,1)}) custom-call(bf16[8,320,896]{2,1,0:T(8,128)(2,1)} %get-tuple-element.12.p_ref, bf16[4,80,896]{2,1,0:T(8,128)(2,1)} %bitcast.58), custom_call_target="tpu_custom_call" | custom-call | flops 22937600 | bytes 229376000 | tf_op jit(solution)/shard_map/exchange/pallas_call | solution.py:445
  111.6 0.0 copy-start.1
  111.6 0.0 copy-start.3
  111.6 0.0 copy-start.5
  111.6 13.8 %back.1 = bf16[320,512]{1,0:T(8,128)(2,1)} custom-call(bf16[8,320,896]{2,1,0:T(8,128)(2,1)} %get-tuple-element.14.dy_ref, bf16[8,320,896]{2,1,0:T(8,128)(2,1)} %get-tuple-element.15.r_ref, bf16[512,7168]{1,0:T(8,128)(2,1)} %bitcast.57, bf16[512,7168]{1,0:T(8,128)(2,1)} %delta.1.delta_ref, bf16[320,512]{1,0:T(8,128)(2,1)} %get-tuple-element.16.s_ref), custom_call_target="tpu_custom_call" | custom-call | flops 4697620480 | bytes 23855104 | tf_op jit(solution)/shard_map/back/pallas_call | solution.py:264
  125.4 3.7 %all-to-all-start.2 = ((bf16[4,80,512]{2,1,0:T(8,128)(2,1)}), bf16[4,80,512]{2,1,0:T(8,128)(2,1)S(1)}, u32[]{:S(2)}, u32[]{:S(2)}) async-start(bf16[4,80,512]{2,1,0:T(8,128)(2,1)} %bitcast.66), calls=%async_computation.2 | async-start | bytes 655360 | tf_op jit(solution)/shard_map/all_to_all | solution.py:537
  129.1 0.0 copy-done.1
  129.1 0.3 convolution_multiply_fusion.2
  129.4 1.0 fusion.2
  130.5 0.0 copy-done.3
  130.5 1.0 copy.51
  131.4 0.0 copy-done.5
  131.4 0.9 copy.52
  132.4 18.2 %grads.1 = (bf16[512,7168]{1,0:T(8,128)(2,1)}, bf16[512,7168]{1,0:T(8,128)(2,1)}) custom-call(bf16[8,320,896]{2,1,0:T(8,128)(2,1)} %get-tuple-element.14.dy_ref, bf16[8,320,896]{2,1,0:T(8,128)(2,1)} %get-tuple-element.15.r_ref, bf16[512,7168]{1,0:T(8,128)(2,1)} %bitcast.53, bf16[512,7168]{1,0:T(8,128)(2,1)} %bitcast.55, bf16[512,320]{1,0:T(8,128)(2,1)} %bitcast.61, ...), custom_call_target="tpu_custom_call" | custom-call | flops 4697620480 | bytes 47710208 | tf_op jit(solution)/shard_map/grads/pallas_call | solution.py:293
  150.6 0.0 all-to-all-done.2
  150.6 0.9 convolution_convert_fusion.1
  (9 shorter events, 0.1 us)
Async XLA Ops:
  0.6 41.6 %copy-start = (bf16[128,896]{1,0:T(8,128)(2,1)S(1)}, bf16[128,896]{1,0:T(8,128)(2,1)}, u32[]{:S(2)}) copy-start(bf16[128,896]{1,0:T(8,128)(2,1)} %param.14) | copy-start | bytes 688132
  8.9 16.7 %all-to-all-start = ((s32[4,80,256]{2,1,0:T(8,128)}), s32[4,80,256]{2,1,0:T(8,128)S(1)}, u32[]{:S(2)}, u32[]{:S(2)}) async-start(s32[4,80,256]{2,1,0:T(8,128)} %bitcast.3), calls=%async_computation | async-start | bytes 655360 | tf_op jit(solution)/shard_map/all_to_all | solution.py:528
  25.6 16.6 %copy-start.4 = (s32[4,80,256]{2,1,0:T(8,128)}, s32[4,80,256]{2,1,0:T(8,128)S(1)}, u32[]{:S(2)}) copy-start(s32[4,80,256]{2,1,0:T(8,128)S(1)} %all-to-all-done) | copy-start | bytes 983044
  25.6 17.8 %all-to-all-start.1 = ((bf16[4,80,512]{2,1,0:T(8,128)(2,1)}), bf16[4,80,512]{2,1,0:T(8,128)(2,1)S(1)}, u32[]{:S(2)}, u32[]{:S(2)}) async-start(bf16[4,80,512]{2,1,0:T(8,128)(2,1)} %bitcast.5), calls=%async_computation.1 | async-start | bytes 655360 | tf_op jit(solution)/shard_map/all_to_all | solution.py:527
  43.4 0.7 copy-start.2
  111.6 17.5 %copy-start.1 = (bf16[4,80,896]{2,1,0:T(8,128)(2,1)S(1)}, bf16[4,80,896]{2,1,0:T(8,128)(2,1)}, u32[]{:S(2)}) copy-start(bf16[4,80,896]{2,1,0:T(8,128)(2,1)} %get-tuple-element.13) | copy-start | bytes 1720324
  111.6 18.9 %copy-start.3 = (bf16[4,80,512]{2,1,0:T(8,128)(2,1)S(1)}, bf16[4,80,512]{2,1,0:T(8,128)(2,1)}, u32[]{:S(2)}) copy-start(bf16[4,80,512]{2,1,0:T(8,128)(2,1)} %copy-done.2) | copy-start | bytes 983044
  111.6 19.9 %copy-start.5 = (bf16[320,512]{1,0:T(8,128)(2,1)S(1)}, bf16[320,512]{1,0:T(8,128)(2,1)}, u32[]{:S(2)}) copy-start(bf16[320,512]{1,0:T(8,128)(2,1)} %get-tuple-element.17) | copy-start | bytes 983044
  125.4 25.2 %all-to-all-start.2 = ((bf16[4,80,512]{2,1,0:T(8,128)(2,1)}), bf16[4,80,512]{2,1,0:T(8,128)(2,1)S(1)}, u32[]{:S(2)}, u32[]{:S(2)}) async-start(bf16[4,80,512]{2,1,0:T(8,128)(2,1)} %bitcast.66), calls=%async_computation.2 | async-start | bytes 655360 | tf_op jit(solution)/shard_map/all_to_all | solution.py:537
where the time goes:
time: 153 us; the launch traced here: 151 us
  Pallas kernels  112 us (73%)
  starting transfers between devices  13.5 us (9%)
  local copies, waits for them, and re-layouts  8.39 us (5%)
  waiting for transfers between devices  7.63 us (5%)
  matrix products  5.28 us (3%)
  other arithmetic  4.07 us (3%)
    pallas_call x1, Pallas kernels, exchange(): pl.pallas_call(exchange_kernel, in_specs=[vmem, vmem], out_specs=[vmem, v...  53.9 us
    pallas_call x1, Pallas kernels, grads(): pl.pallas_call(grads_kernel, grid=(parts,), in_specs=[piece, piece, weigh...  18.2 us
    pallas_call x1, Pallas kernels, back(): pl.pallas_call(back_kernel, grid=(parts,), in_specs=[piece, piece, weight...  13.8 us
    pallas_call x1, Pallas kernels, forward(): pl.pallas_call(functools.partial(forward_kernel, in_words), grid=(parts,)...  13.5 us
    pallas_call x1, Pallas kernels, make_delta(): pl.pallas_call(delta_kernel, grid=(width // rows,), in_specs=[spec, spec]...  12.4 us
    all_to_all x1, waiting for transfers between devices, on_device(): recv_words = swap(send_words).reshape(slots, -1)  7.63 us
    all_to_all x1, starting transfers between devices, on_device(): recv_words = swap(send_words).reshape(slots, -1)  6.35 us
    dot_general x5, matrix products, exact_dot(): return jnp.dot(onehot, values, preferred_element_type=jnp.float32)  5.28 us
  transfers between devices with their start and end apart: 3, of which 1 were waited for; matrix products, arithmetic and copies ran while one was open for 5% of the time, Pallas kernels for 20%

commit v1 on v0

v1 whole, which is shorter than its diff:
```python
import functools

import jax
import jax.numpy as jnp
from jax import lax
from jax.experimental import pallas as pl
from jax.experimental.pallas import tpu as pltpu
from jax.sharding import PartitionSpec as P

def unpack_rows(words):
    shifts = jnp.arange(32, dtype=jnp.int32)
    bits = jnp.bitwise_and(jnp.right_shift(words[..., None], shifts), 1)
    signs = (1 - 2 * bits).astype(jnp.float32)
    return signs.reshape(words.shape[:-1] + (words.shape[-1] * 32,))


def unpack_cols(words):
    shifts = jnp.arange(32, dtype=jnp.int32)
    bits = jnp.bitwise_and(jnp.right_shift(words.T[:, None, :], shifts[None, :, None]), 1)
    signs = (1 - 2 * bits).astype(jnp.float32)
    return signs.reshape(words.shape[1] * 32, words.shape[0])


def block_slots(block_ids, experts, capacity):
    onehot = (block_ids[:, :, None] == jnp.arange(experts, dtype=jnp.int32)).astype(jnp.int32)
    flat = onehot.reshape(-1, experts)
    before = jnp.cumsum(flat, axis=0) - flat
    ranks = jnp.sum(before * flat, axis=1).reshape(block_ids.shape)
    return block_ids * capacity + ranks


def on_device_general(
    tokens,
    in_signs,
    out_signs,
    expert_ids,
    route_weight,
    cotangent,
    mean_weight,
    rho_weight,
    noise_weight,
):
    experts = lax.axis_size("expert") * mean_weight.shape[0]
    token_count = tokens.shape[0]
    topk = expert_ids.shape[1]
    capacity = 5 * token_count * topk // (4 * experts)
    slots = experts * capacity
    width_local = tokens.shape[1]
    sign_words = in_signs.shape[1]
    hidden_local = cotangent.shape[1]
    slot_of = block_slots(expert_ids, experts, capacity)
    match = (slot_of[:, :, None] == jnp.arange(slots, dtype=jnp.int32)).astype(jnp.int32)
    token_rank = jnp.arange(token_count, dtype=jnp.int32)[:, None, None]
    slot_token = jnp.sum(match * token_rank, axis=(0, 1))
    slot_fill = jnp.sum(match, axis=(0, 1))
    slot_weight = jnp.sum(match.astype(jnp.float32) * route_weight[:, :, None], axis=(0, 1))
    words = jnp.concatenate([in_signs, out_signs], axis=1)
    fill_rows = slot_fill.astype(jnp.bfloat16)[:, None]
    send_rows = (jnp.take(tokens, slot_token, axis=0) * fill_rows).reshape(
        experts, capacity, width_local
    )
    send_words = jnp.take(words, slot_token, axis=0).reshape(experts, capacity, words.shape[1])
    recv_rows, recv_words = (
        lax.all_to_all(send_rows, "expert", split_axis=0, concat_axis=0, tiled=True),
        lax.all_to_all(send_words, "expert", split_axis=0, concat_axis=0, tiled=True),
    )
    rows = recv_rows.reshape(slots, width_local)
    recv_words = recv_words.reshape(slots, words.shape[1])
    input_signs = unpack_rows(recv_words[:, :sign_words])
    input_cols = unpack_cols(recv_words[:, :sign_words])
    signed = rows * input_signs.astype(jnp.bfloat16)
    mean_local = mean_weight[0]
    rho_float = rho_weight[0].astype(jnp.float32)
    noise_float = noise_weight[0].astype(jnp.float32)
    delta = (jax.nn.softplus(rho_float) * noise_float).astype(jnp.bfloat16)
    contract = (((0,), (1,)), ((), ()))
    output_cols = unpack_cols(recv_words[:, sign_words:])
    mean_cols = mean_local
    delta_cols = delta
    mean_part = lax.dot_general(mean_cols, rows, contract, preferred_element_type=jnp.float32)
    pert_part = lax.dot_general(delta_cols, signed, contract, preferred_element_type=jnp.float32)
    mean_part, pert_part = (mean_part, pert_part)
    preact = lax.psum_scatter(
        mean_part + output_cols * pert_part, "dp", scatter_dimension=0, tiled=True
    )
    gate = jax.nn.sigmoid(preact)
    hidden_slots = (preact * gate).astype(jnp.bfloat16)
    slope = gate * (1.0 + preact * (1.0 - gate))
    returned = lax.all_to_all(
        hidden_slots.reshape(hidden_local, experts, capacity),
        "expert",
        split_axis=1,
        concat_axis=1,
        tiled=True,
    )
    returned = returned.reshape(hidden_local, slots)
    picked = jnp.take(returned, slot_of, axis=1).astype(jnp.float32)
    hidden_out = jnp.sum(picked * route_weight[None], axis=2).T.astype(jnp.bfloat16)
    upstream = jnp.take(cotangent.T, slot_token, axis=1).astype(jnp.float32) * slot_weight[None, :]
    upstream = upstream.astype(jnp.bfloat16).reshape(hidden_local, experts, capacity)
    arrived = lax.all_to_all(upstream, "expert", split_axis=1, concat_axis=1, tiled=True).reshape(
        hidden_local, slots
    )
    grad_preact = (arrived.astype(jnp.float32) * slope).astype(jnp.bfloat16)
    piece = lax.all_gather(grad_preact, "dp", axis=0, tiled=True)
    piece_signed = piece * output_cols.astype(jnp.bfloat16)
    mean_cols = mean_local
    delta_cols = delta
    grad_rows = jnp.dot(mean_cols, piece, preferred_element_type=jnp.float32)
    grad_signed = jnp.dot(delta_cols, piece_signed, preferred_element_type=jnp.float32)
    mean_block = lax.dot_general(rows, piece, contract, preferred_element_type=jnp.float32)
    delta_block = lax.dot_general(
        signed, piece_signed, contract, preferred_element_type=jnp.float32
    )
    grad_mean_acc = mean_block
    grad_delta_acc = delta_block
    result = (grad_rows, grad_signed, grad_mean_acc, grad_delta_acc)
    grad_rows, grad_signed, grad_mean_acc, grad_delta_acc = result
    slot_grad = (grad_rows + input_cols * grad_signed).astype(jnp.bfloat16)
    back = lax.all_to_all(
        slot_grad.reshape(width_local, experts, capacity),
        "expert",
        split_axis=1,
        concat_axis=1,
        tiled=True,
    )
    back = back.reshape(width_local, slots)
    grad_tokens = jnp.sum(jnp.take(back, slot_of, axis=1).astype(jnp.float32), axis=2).T.astype(
        jnp.bfloat16
    )
    grad_mean = grad_mean_acc.astype(jnp.bfloat16)[None]
    grad_rho = (grad_delta_acc * noise_float * jax.nn.sigmoid(rho_float)).astype(jnp.bfloat16)[None]
    return (hidden_out, grad_tokens, grad_mean, grad_rho)


LANES = 128
VMEM_LIMIT = 60 * 1024 * 1024
RANKS = 4
COPIES = 80
NT = (((1,), (1,)), ((), ()))
TN = (((0,), (0,)), ((), ()))
ORDER = (7, 6, 3, 2, 5, 4, 1, 0)


def dot(a, b, dims=None):
    if dims is None:
        return jnp.dot(a, b, preferred_element_type=jnp.float32)
    return lax.dot_general(a, b, dims, preferred_element_type=jnp.float32)


def total(*terms):
    out = terms[0].astype(jnp.float32)
    for term in terms[1:]:
        out = out + term.astype(jnp.float32)
    return out


def signs_of(words, first, tiles):
    rows = words.shape[0]
    lane = lax.broadcasted_iota(jnp.int32, (rows, LANES), 1)
    shift = lane % 32
    out = []
    for tile in range(tiles):
        at = first + 4 * tile + lane // 32
        picked = jnp.take_along_axis(words, at, axis=1, mode="promise_in_bounds")
        bits = jnp.bitwise_and(jnp.right_shift(picked, shift), 1)
        out.append((1 - 2 * bits).astype(jnp.float32).astype(jnp.bfloat16))
    return jnp.concatenate(out, axis=1) if tiles > 1 else out[0]


def step_kernel(
    ids_ref, weight_ref, tok_ref, cot_ref, inw_ref, outw_ref, mean_hbm, rho_hbm, noise_hbm,
    hid_ref, fill_ref, g_ref, at_ref, bt_ref, dy_hbm, dyr_hbm, q_hbm,
    mean_v, delta_v, q_v, part, r_v, dy_v, rd, cs, land, xs, bs, ss, send_x,
    words_s, words_v, raw, up_s, up_v, h_s, h_v, one_v, plain, signed,
    send_sem, recv_sem, local_sem,
):
    bf16, f32 = jnp.bfloat16, jnp.float32
    me = lax.axis_index("dp")
    mine = lax.axis_index("expert")
    tokens = tok_ref.shape[0]
    width = tok_ref.shape[1]
    block = cot_ref.shape[1]
    cap = up_v.shape[1]
    pair = 2 * cap
    slots = RANKS * cap
    in_words = inw_ref.shape[0]
    half_words = outw_ref.shape[0] // 2
    piece_words = block // 32
    y, x, c = me // 4, (me // 2) % 2, me % 2
    place = lambda dy, dx, dc: ((y + dy) % 2) * 4 + ((x + dx) % 2) * 2 + (c + dc) % 2
    owner = [place(l // 4, (l // 2) % 2, l % 2) for l in range(8)]
    at_x, at_y, at_c = (place(0, 1, 0), mine), (place(1, 0, 0), mine), (place(0, 0, 1), mine)
    zs = [mine, mine + 1 - 2 * (mine % 2), (mine + 2) % 4, 3 - mine]
    at_z = [(me, z) for z in zs]
    count = [0, 0]
    started, copied = [], []

    def send(src, dst, to):
        n = count[0]
        count[0] += 1
        copy = pltpu.make_async_remote_copy(
            src_ref=src,
            dst_ref=dst,
            send_sem=send_sem.at[n],
            recv_sem=recv_sem.at[n],
            device_id=to,
            device_id_type=pl.DeviceIdType.MESH,
        )
        copy.start()
        started.append(copy)
        return copy

    def local(src, dst, keep=True):
        n = count[1]
        count[1] += 1
        copy = pltpu.make_async_copy(src, dst, local_sem.at[n])
        copy.start()
        if keep:
            copied.append(copy)
        return copy

    cols = [pl.ds(pl.multiple_of(owner[l] * block, LANES), block) for l in range(8)]
    got = {}
    for l in ORDER:
        got[l] = (
            local(rho_hbm.at[:, cols[l]], delta_v.at[l], False),
            local(noise_hbm.at[:, cols[l]], q_v.at[l], False),
            local(mean_hbm.at[:, cols[l]], mean_v.at[l], False),
        )

    barrier = pltpu.get_barrier_semaphore()
    peers = [at_x, at_y, at_c] + at_z[1:]
    for peer in peers:
        pl.semaphore_signal(barrier, inc=1, device_id=peer, device_id_type=pl.DeviceIdType.MESH)

    ids = ids_ref[...]
    weight = weight_ref[...]
    id0, id1 = ids[0:1, :], ids[1:2, :]
    w0, w1 = weight[0:1, :], weight[1:2, :]
    sub16 = lax.broadcasted_iota(jnp.int32, (16, tokens), 0)
    named = jnp.zeros((16, tokens), f32)
    for j in range(RANKS):
        hit = jnp.where(id0 == zs[j], 1.0, 0.0) + jnp.where(id1 == zs[j], 1.0, 0.0)
        named = jnp.where(sub16 == j, jnp.broadcast_to(hit, (16, tokens)), named)
    row_at = lax.broadcasted_iota(jnp.int32, (tokens, tokens), 0)
    col_at = lax.broadcasted_iota(jnp.int32, (tokens, tokens), 1)
    earlier = jnp.where(row_at < col_at, 1.0, 0.0).astype(bf16)
    ranks = dot(named.astype(bf16), earlier)
    slot_at = lax.broadcasted_iota(jnp.int32, (cap, tokens), 0).astype(f32)
    slot_weight = []
    for j in range(RANKS):
        rows = pl.ds(j * cap, cap)
        here = jnp.where(slot_at == ranks[j : j + 1, :], 1.0, 0.0)
        one = here * jnp.where(id0 == zs[j], 1.0, 0.0)
        two = here * jnp.where(id1 == zs[j], 1.0, 0.0)
        one_v[0, rows] = one.astype(bf16)
        one_v[1, rows] = two.astype(bf16)
        fill_ref[rows] = (one + two).astype(bf16)
        slot_weight.append(jnp.sum(one * w0 + two * w1, axis=1, keepdims=True))
    fill = fill_ref[...]
    taken = dot(fill, tok_ref[...]).astype(bf16)
    xs[pl.ds(0, cap)] = taken[:cap]
    send_x[...] = taken
    words_s[pl.ds(0, half_words)] = outw_ref[pl.ds(pl.multiple_of(c * half_words, 8), half_words)]
    words_s[pl.ds(half_words, in_words)] = inw_ref[...]
    words = words_s[...]
    gathered = None
    for k in range(4):
        plane = jnp.bitwise_and(jnp.right_shift(words, 8 * k), 255).astype(f32).astype(bf16)
        got_plane = jnp.left_shift(dot(fill, plane, NT).astype(jnp.int32), 8 * k)
        gathered = got_plane if k == 0 else jnp.bitwise_or(gathered, got_plane)
    raw[...] = gathered
    words_v[c, pl.ds(0, cap)] = gathered[:cap]

    pl.semaphore_wait(barrier, len(peers))
    block_rows = [pl.ds(j * cap, cap) for j in range(RANKS)]
    pair_rows = [pl.ds(0, pair), pl.ds(pair, pair)]
    x_in, w_in, w_swap, up_in = {}, {}, {}, {}

    def send_rows(j):
        x_in[j] = send(send_x.at[block_rows[j]], xs.at[block_rows[j]], at_z[j])

    def send_words(j):
        w_in[j] = send(raw.at[block_rows[j]], words_v.at[c, block_rows[j]], at_z[j])

    def swap_words(j):
        here = words_v.at[c, block_rows[j]]
        w_swap[j] = send(here, here, at_c)

    send_rows(1)
    send_words(1)
    send_rows(2)
    send_rows(3)
    send_words(2)
    send_words(3)
    swap_words(0)

    def make_delta(l):
        got[l][0].wait()
        got[l][1].wait()

        @pl.loop(0, width // 32)
        def _(i):
            rows = pl.ds(pl.multiple_of(i * 32, 32), 32)
            rho = delta_v[l, rows].astype(f32)
            noise = q_v[l, rows].astype(f32)
            soft = jnp.log(1.0 + jnp.exp(rho))
            delta_v[l, rows] = (soft * noise).astype(bf16)
            q_v[l, rows] = (jnp.exp(rho - soft) * noise).astype(bf16)

    for l in ORDER[:3]:
        make_delta(l)
    up = dot(fill, cot_ref[...])
    for j in range(RANKS):
        mixed = (up[j * cap : (j + 1) * cap] * slot_weight[j]).astype(bf16)
        if j == 0:
            up_v[0] = mixed
        else:
            up_s[j] = mixed
    for j in range(1, RANKS):
        up_in[j] = send(up_s.at[j], up_v.at[j], at_z[j])
    for l in ORDER[3:5]:
        make_delta(l)
    made = set(ORDER[:5])

    def arrive(p):
        blocks = (1,) if p == 0 else (2, 3)
        for j in blocks:
            x_in[j].wait_recv()
            w_in[j].wait_recv()
            swap_words(j)
        rows = pair_rows[p]
        signs = signs_of(words_v[c, rows], half_words, width // LANES)
        ss[rows] = signs
        bs[rows] = xs[rows] * signs
        for j in (2 * p, 2 * p + 1):
            w_swap[j].wait_recv()

    def forward(p, l):
        rows = pair_rows[p]
        if l not in made:
            make_delta(l)
            made.add(l)
        if p == 0:
            got[l][2].wait()
        one = dot(xs[rows], mean_v[l])
        two = dot(bs[rows], delta_v[l])
        signs = signs_of(
            words_v[owner[l] // 4, rows], (owner[l] % 4) * piece_words, block // LANES
        )
        r_v[l, rows] = signs
        part[l, rows] = (one + signs.astype(f32) * two).astype(bf16)

    core, sent = {}, {}

    def to_core(p, k):
        rows = pair_rows[p]
        core[p, k] = send(part.at[2 * k + 1, rows], rd.at[k, rows], at_c)

    def hop(p, k, which, name, to, extra=None):
        rows = block_rows[2 * p + which]
        terms = [part[2 * k, rows], rd[k, rows]]
        if extra is not None:
            terms.append(land[p, extra])
        cs[k, rows] = total(*terms).astype(bf16)
        sent[p, name] = send(cs.at[k, rows], land.at[p, name], to)

    D_X, D_Y, N_X, N_Y, L_Y, L_X = range(6)

    def reduce_first(p, middle):
        forward(p, 7)
        to_core(p, 3)
        forward(p, 6)
        core[p, 3].wait_recv()
        hop(p, 3, 0, D_X, at_x)
        hop(p, 3, 1, D_Y, at_y)
        forward(p, 3)
        to_core(p, 1)
        forward(p, 2)
        core[p, 1].wait_recv()
        hop(p, 1, 0, N_X, at_x)
        forward(p, 5)
        to_core(p, 2)
        forward(p, 4)
        core[p, 2].wait_recv()
        hop(p, 2, 1, N_Y, at_y)
        middle()
        forward(p, 1)
        to_core(p, 0)
        forward(p, 0)

    def reduce_last(p):
        sent[p, D_X].wait_recv()
        hop(p, 2, 0, L_Y, at_y, D_X)
        sent[p, D_Y].wait_recv()
        hop(p, 1, 1, L_X, at_x, D_Y)
        core[p, 0].wait_recv()

    spread, h_in = {}, {}

    def pass_on(p, which, l, to_l, to, name):
        rows = block_rows[2 * p + which]
        spread[p, name] = send(dy_v.at[l, rows], dy_v.at[to_l, rows], to)

    def activate(p, which):
        j = 2 * p + which
        rows = block_rows[j]
        if j > 0:
            up_in[j].wait_recv()
        near, last = (N_X, L_Y) if which == 0 else (N_Y, L_X)
        sent[p, near].wait_recv()
        sent[p, last].wait_recv()
        preact = total(part[0, rows], rd[0, rows], land[p, near], land[p, last])
        gate = 1.0 / (1.0 + jnp.exp(-preact))
        hidden = (preact * gate).astype(bf16)
        slope = gate * (1.0 + preact * (1.0 - gate))
        dy_v[0, rows] = (up_v[j].astype(f32) * slope).astype(bf16)
        if j == 0:
            h_v[0] = hidden
        else:
            h_s[j] = hidden

    def gather_first(p):
        activate(p, 0)
        pass_on(p, 0, 0, 4, at_y, "y1")
        pass_on(p, 0, 0, 2, at_x, "x2")
        pass_on(p, 0, 0, 1, at_c, "c0")
        activate(p, 1)
        pass_on(p, 1, 0, 2, at_x, "x1")
        pass_on(p, 1, 0, 4, at_y, "y2")
        pass_on(p, 1, 0, 1, at_c, "c1")
        for j in (2 * p, 2 * p + 1):
            if j > 0:
                h_in[j] = send(h_s.at[j], h_v.at[j], at_z[j])

    def gather_relay(p):
        spread[p, "y1"].wait_recv()
        pass_on(p, 0, 4, 6, at_x, "x3")
        pass_on(p, 0, 4, 5, at_c, "c2")
        spread[p, "x1"].wait_recv()
        pass_on(p, 1, 2, 6, at_y, "y3")
        pass_on(p, 1, 2, 3, at_c, "c3")

    def gather_near(p):
        spread[p, "x2"].wait_recv()
        pass_on(p, 0, 2, 3, at_c, "c4")
        spread[p, "y2"].wait_recv()
        pass_on(p, 1, 4, 5, at_c, "c5")

    def gather_last(p):
        spread[p, "x3"].wait_recv()
        pass_on(p, 0, 6, 7, at_c, "c6")
        spread[p, "y3"].wait_recv()
        pass_on(p, 1, 6, 7, at_c, "c7")

    first_back = {0: True, 1: True}

    def back(p, l, waits=()):
        for name in waits:
            spread[p, name].wait_recv()
        rows = pair_rows[p]
        dy = dy_v[l, rows]
        dyr = dy * r_v[l, rows]
        r_v[l, rows] = dyr
        one = dot(dy, mean_v[l], NT)
        two = dot(dyr, delta_v[l], NT)
        if first_back[p]:
            plain[rows] = one
            signed[rows] = two
            first_back[p] = False
        else:
            plain[rows] += one
            signed[rows] += two
        if p == 1:
            local(dy_v.at[l], dy_hbm.at[:, cols[l]])
            local(r_v.at[l], dyr_hbm.at[:, cols[l]])

    arrive(0)
    reduce_first(0, lambda: None)
    reduce_last(0)
    for l in range(8):
        local(q_v.at[l], q_hbm.at[:, cols[l]])
    arrive(1)
    reduce_first(1, lambda: gather_first(0))
    reduce_last(1)
    at_ref[...] = xs[...].T
    bt_ref[...] = bs[...].T
    back(0, 0)
    back(0, 1, ("c0", "c1"))
    gather_relay(0)
    gather_first(1)
    gather_near(0)
    back(0, 2)
    back(0, 4)
    back(0, 3, ("c3", "c4"))
    back(0, 5, ("c2", "c5"))
    back(1, 0)
    back(1, 1, ("c0", "c1"))
    gather_last(0)
    back(0, 6)
    back(0, 7, ("c6", "c7"))
    gather_relay(1)
    gather_near(1)
    back(1, 2)
    back(1, 4)
    back(1, 3, ("c3", "c4"))
    back(1, 5, ("c2", "c5"))
    for j in range(1, RANKS):
        h_in[j].wait_recv()
    out = None
    for k, w in enumerate((w0, w1)):
        column = jnp.sum(jnp.where(row_at == col_at, w, 0.0), axis=1, keepdims=True)
        picked = None
        for j in range(RANKS):
            one = dot(one_v[k, block_rows[j]], h_v[j], TN)
            picked = one if picked is None else picked + one
        picked = picked * column
        out = picked if out is None else out + picked
    hid_ref[...] = out.astype(bf16)
    gather_last(1)
    back(1, 6)
    back(1, 7, ("c6", "c7"))
    g_ref[...] = (plain[...] + ss[...].astype(f32) * signed[...]).astype(bf16)
    for copy in started:
        copy.wait_send()
    for copy in copied:
        copy.wait()


def run_step(ids, weight, tokens, cotangent, in_words, out_words, mean, rho, noise, cap):
    bf16, f32 = jnp.bfloat16, jnp.float32
    width, hidden = mean.shape
    count = tokens.shape[0]
    block = cotangent.shape[1]
    slots = RANKS * cap
    vmem = pl.BlockSpec(memory_space=pltpu.VMEM)
    hbm = pl.BlockSpec(memory_space=pltpu.MemorySpace.HBM)
    shape = jax.ShapeDtypeStruct
    weights = pltpu.VMEM((8, width, block), bf16)
    piece = pltpu.VMEM((8, slots, block), bf16)
    four = pltpu.VMEM((4, slots, block), bf16)
    small = pltpu.VMEM((slots, width), bf16)
    per = pltpu.VMEM((RANKS, cap, block), bf16)
    macs = slots * width * hidden
    return pl.pallas_call(
        step_kernel,
        in_specs=[vmem] * 6 + [hbm] * 3,
        out_specs=[vmem] * 5 + [hbm] * 3,
        out_shape=[
            shape((count, block), bf16),
            shape((slots, count), bf16),
            shape((slots, width), bf16),
            shape((width, slots), bf16),
            shape((width, slots), bf16),
            shape((slots, hidden), bf16),
            shape((slots, hidden), bf16),
            shape((width, hidden), bf16),
        ],
        scratch_shapes=[
            weights, weights, weights, piece, piece, piece, four, four,
            pltpu.VMEM((2, 6, cap, block), bf16),
            small, small, small, small,
            pltpu.VMEM((LANES, count), jnp.int32),
            pltpu.VMEM((2, slots, LANES), jnp.int32),
            pltpu.VMEM((slots, LANES), jnp.int32),
            per, per, per, per,
            pltpu.VMEM((2, slots, count), bf16),
            pltpu.VMEM((slots, width), f32),
            pltpu.VMEM((slots, width), f32),
            pltpu.SemaphoreType.DMA((COPIES,)),
            pltpu.SemaphoreType.DMA((COPIES,)),
            pltpu.SemaphoreType.DMA((COPIES,)),
        ],
        compiler_params=pltpu.CompilerParams(
            collective_id=0, has_side_effects=True, vmem_limit_bytes=VMEM_LIMIT
        ),
        cost_estimate=pl.CostEstimate(
            flops=8 * macs, bytes_accessed=10 * width * hidden, transcendentals=3 * width * hidden
        ),
        name="step",
    )(ids, weight, tokens, cotangent, in_words, out_words, mean, rho, noise)


def grads_kernel(dy_ref, dyr_ref, q_ref, at_ref, bt_ref, gm_ref, gr_ref):
    gm_ref[...] = dot(at_ref[...], dy_ref[...]).astype(gm_ref.dtype)
    gd = dot(bt_ref[...], dyr_ref[...])
    gr_ref[...] = (gd * q_ref[...].astype(jnp.float32)).astype(gr_ref.dtype)


def grads(dy, dyr, q, at, bt, block):
    slots, hidden = dy.shape
    width = q.shape[0]
    weight = pl.BlockSpec((width, block), lambda i: (0, i))
    piece = pl.BlockSpec((slots, block), lambda i: (0, i))
    whole = pl.BlockSpec((width, slots), lambda i: (0, 0))
    out = jax.ShapeDtypeStruct((width, hidden), jnp.bfloat16)
    return pl.pallas_call(
        grads_kernel,
        grid=(hidden // block,),
        in_specs=[piece, piece, weight, whole, whole],
        out_specs=[weight, weight],
        out_shape=[out, out],
        compiler_params=pltpu.CompilerParams(
            dimension_semantics=("arbitrary",), vmem_limit_bytes=40 * 1024 * 1024
        ),
        cost_estimate=pl.CostEstimate(
            flops=4 * slots * width * hidden,
            bytes_accessed=hidden * (6 * width + 4 * slots),
            transcendentals=0,
        ),
        name="grads",
    )(dy, dyr, q, at, bt)


def on_device(
    tokens,
    in_signs,
    out_signs,
    expert_ids,
    route_weight,
    cotangent,
    mean_weight,
    rho_weight,
    noise_weight,
):
    parts = lax.axis_size("dp")
    ranks = lax.axis_size("expert")
    count, width = tokens.shape
    topk = expert_ids.shape[1]
    hidden = mean_weight.shape[2]
    block = cotangent.shape[1]
    capacity = 5 * count * topk // (4 * ranks)
    half = out_signs.shape[1] // 2
    fits = parts == 8 and ranks == RANKS and mean_weight.shape[0] == 1 and topk == 2
    fits = fits and block % LANES == 0 and width % LANES == 0 and count == LANES
    fits = fits and half + in_signs.shape[1] == LANES and half % 8 == 0 and capacity % 16 == 0
    if not fits or hidden % 512:
        return on_device_general(
            tokens,
            in_signs,
            out_signs,
            expert_ids,
            route_weight,
            cotangent,
            mean_weight,
            rho_weight,
            noise_weight,
        )
    hidden_out, fill, g, at, bt, dy, dyr, q = run_step(
        expert_ids.T,
        route_weight.T,
        tokens,
        cotangent,
        in_signs.T,
        out_signs.T,
        mean_weight[0],
        rho_weight[0],
        noise_weight[0],
        capacity,
    )
    pieces = [g[:capacity]]
    for j in range(1, ranks):
        swap = [(z, z ^ j) for z in range(ranks)]
        pieces.append(lax.ppermute(g[j * capacity : (j + 1) * capacity], "expert", swap))
    grad_mean, grad_rho = grads(dy, dyr, q, at, bt, 512)
    g_back = jnp.concatenate(pieces, axis=0)
    grad_tokens = dot(fill, g_back, TN).astype(jnp.bfloat16)
    return (hidden_out, grad_tokens, grad_mean[None], grad_rho[None])


def solution(mesh):
    in_specs = (
        P("expert", "dp"),
        P("expert", "dp"),
        P("expert", None),
        P("expert", None),
        P("expert", None),
        P("expert", "dp"),
        P("expert", "dp", None),
        P("expert", "dp", None),
        P("expert", "dp", None),
    )
    out_specs = (
        P("expert", "dp"),
        P("expert", "dp"),
        P("expert", "dp", None),
        P("expert", "dp", None),
    )
    return jax.shard_map(
        on_device, mesh=mesh, in_specs=in_specs, out_specs=out_specs, check_vma=False
    )
```

time: 153 us -> 95.1 us (0.62)
  Pallas kernels: 112 us -> 80.1 us
  starting transfers between devices: 13.5 us -> 4.45 us
  waiting for transfers between devices: 7.63 us -> 0.01 us
  matrix products: 5.28 us -> 0.91 us
  other arithmetic: 4.07 us -> 0 us
    pallas_call x5 -> x2, Pallas kernels: 112 us -> 80.1 us  [the longest x1 64.7 us: run_step(): pl.pallas_call(step_kernel, in_specs=[vmem] * 6 + [hbm] * 3, out_specs=[v...]
    all_to_all x3 -> x0, starting transfers between devices: 13.5 us -> none  [the longest x1 6.35 us: on_device(): recv_words = swap(send_words).reshape(slots, -1)]
    all_to_all x3 -> x0, waiting for transfers between devices: 7.63 us -> none  [the longest x1 7.63 us: on_device(): recv_words = swap(send_words).reshape(slots, -1)]
    ppermute x0 -> x3, starting transfers between devices: none -> 4.45 us  [on_device(): lax.ppermute(g[j * capacity:(j + 1) * capacity], 'expert', swap)]
    dot_general x5 -> x1, matrix products: 5.28 us -> 0.91 us  [dot(): return lax.dot_general(a, b, dims, preferred_element_type=jnp.float32)]
    unnamed x15 -> x13, local copies, waits for them, and re-layouts: 3.37 us -> 7.28 us
    gather x1 -> x0, local copies, waits for them, and re-layouts: 1.63 us -> none  [on_device(): jnp.take(words, slot_token, axis=0).reshape(experts, capacity, -1)]
  transfers between devices with their start and end apart: 3 -> 3, of which waited for: 1 -> 0; matrix products, arithmetic and copies ran while one was open for 5% -> 0% of each run, Pallas kernels for 20% -> 16%
where the time goes in v1:
time: 95.1 us; the launch traced here: 94.4 us
  Pallas kernels  80.1 us (84%)
  local copies, waits for them, and re-layouts  8.31 us (9%)
  starting transfers between devices  4.45 us (5%)
    pallas_call x1, Pallas kernels, run_step(): pl.pallas_call(step_kernel, in_specs=[vmem] * 6 + [hbm] * 3, out_specs=[v...  64.7 us
    pallas_call x1, Pallas kernels, grads(): pl.pallas_call(grads_kernel, grid=(hidden // block,), in_specs=[piece, pi...  15.4 us
    unnamed x13, local copies, waits for them, and re-layouts  7.28 us
    ppermute x3, starting transfers between devices, on_device(): lax.ppermute(g[j * capacity:(j + 1) * capacity], 'expert', swap)  4.45 us
  transfers between devices with their start and end apart: 3, of which 0 were waited for; matrix products, arithmetic and copies ran while one was open for 0% of the time, Pallas kernels for 16%

profile of v1, /device:TPU:0, one launch (start us, length us, event | category | flops | bytes accessed | tf_op | source)
XLA Modules:
  0.0 94.4 jit_solution(13550198192177953135)
XLA Ops:
  0.6 64.7 %step.1 = (bf16[128,896]{1,0:T(8,128)(2,1)}, bf16[320,128]{1,0:T(8,128)(2,1)}, bf16[320,512]{1,0:T(8,128)(2,1)}, bf16[512,320]{1,0:T(8,128)(2,1)}, bf16[512,320]...) custom-call(s32[2,128]{1,0:T(2,128)} %bitcast.15, ...), custom_call_target="tpu_custom_call" | custom-call | flops 9395240960 | bytes 36700160 | tf_op jit(solution)/shard_map/step/pallas_call | solution.py:546
  65.3 1.0 %fusion.8 = (bf16[80,512]{1,0:T(8,128)(2,1)S(1)}, bf16[80,512]{1,0:T(8,128)(2,1)S(1)}, bf16[80,512]{1,0:T(8,128)(2,1)S(1)}, bf16[80,512]{1,0:T(8,128)(2,1)S(1)}) fusion(bf16[320,512]{1,0:T(8,128)(2,1)} %get-tuple-element.16), kind=kLoop, calls=%fused_computation.9 | loop fusion | bytes 655360 | tf_op jit(solution)/shard_map/slice | solution.py:662
  66.4 1.2 %collective-permute-start.2 = (bf16[80,512]{1,0:T(8,128)(2,1)S(1)}, bf16[80,512]{1,0:T(8,128)(2,1)S(1)}, u32[]{:S(2)}, u32[]{:S(2)}) collective-permute-start(bf16[80,512]{1,0:T(8,128)(2,1)S(1)} %get-tuple-element.25), channel_id=1, source_target_pairs={{0,3},{1,2},{2,1},{3,0},{4,7},{5,6},{6,5},{7,4},{8,11},{9,10},{10,... | collective-permute-start | bytes 245768 | tf_op jit(solution)/shard_map/ppermute | solution.py:665
  67.6 1.0 %collective-permute-start.1 = (bf16[80,512]{1,0:T(8,128)(2,1)S(1)}, bf16[80,512]{1,0:T(8,128)(2,1)S(1)}, u32[]{:S(2)}, u32[]{:S(2)}) collective-permute-start(bf16[80,512]{1,0:T(8,128)(2,1)S(1)} %get-tuple-element.26), channel_id=1, source_target_pairs={{0,2},{1,3},{2,0},{3,1},{4,6},{5,7},{6,4},{7,5},{8,10},{9,11},{10,... | collective-permute-start | bytes 245768 | tf_op jit(solution)/shard_map/ppermute | solution.py:665
  68.6 2.3 %collective-permute-start = (bf16[80,512]{1,0:T(8,128)(2,1)S(1)}, bf16[80,512]{1,0:T(8,128)(2,1)S(1)}, u32[]{:S(2)}, u32[]{:S(2)}) collective-permute-start(bf16[80,512]{1,0:T(8,128)(2,1)S(1)} %get-tuple-element.27), channel_id=1, source_target_pairs={{0,1},{1,0},{2,3},{3,2},{4,5},{5,4},{6,7},{7,6},{8,9},{9,8},{10,11... | collective-permute-start | bytes 245768 | tf_op jit(solution)/shard_map/ppermute | solution.py:665
  70.8 0.0 copy-start
  70.8 2.3 %copy-done = bf16[320,7168]{1,0:T(8,128)(2,1)S(1)} copy-done((bf16[320,7168]{1,0:T(8,128)(2,1)S(1)}, bf16[320,7168]{1,0:T(8,128)(2,1)}, u32[]{:S(2)}) %copy-start) | copy-done | bytes 4587544
  73.1 0.0 copy-start.1
  73.1 2.3 %copy-done.1 = bf16[320,7168]{1,0:T(8,128)(2,1)S(1)} copy-done((bf16[320,7168]{1,0:T(8,128)(2,1)S(1)}, bf16[320,7168]{1,0:T(8,128)(2,1)}, u32[]{:S(2)}) %copy-start.1) | copy-done | bytes 4587544
  75.4 0.0 copy-start.2
  75.4 1.0 %copy-done.2 = bf16[512,320]{1,0:T(8,128)(2,1)S(1)} copy-done((bf16[512,320]{1,0:T(8,128)(2,1)S(1)}, bf16[512,320]{1,0:T(8,128)(2,1)}, u32[]{:S(2)}) %copy-start.2) | copy-done | bytes 327704
  76.4 0.0 copy-start.3
  76.4 1.0 %copy-done.3 = bf16[512,320]{1,0:T(8,128)(2,1)S(1)} copy-done((bf16[512,320]{1,0:T(8,128)(2,1)S(1)}, bf16[512,320]{1,0:T(8,128)(2,1)}, u32[]{:S(2)}) %copy-start.3) | copy-done | bytes 327704
  77.4 0.0 copy-start.5
  77.4 0.0 copy-start.4
  77.4 15.4 %grads.1 = (bf16[512,7168]{1,0:T(8,128)(2,1)}, bf16[512,7168]{1,0:T(8,128)(2,1)}) custom-call(bf16[320,7168]{1,0:T(8,128)(2,1)S(1)} %copy-done, bf16[320,7168]{1,0:T(8,128)(2,1)S(1)} %copy-done.1, bf16[512,7168]{1,0:T(8,128)(2,1)} %get-tuple-element.19.q_ref, bf16[512,320]{1,0:T(8,128)(2,1)S(1)} %copy-done.2, bf16[512,320]{1,0:T(8,128)(2,1)S(1)} %copy-done.3), custom_call_target="tpu_custom_call" | custom-call | flops 4697620480 | bytes 31195136 | tf_op jit(solution)/shard_map/grads/pallas_call | solution.py:598
  92.8 0.0 collective-permute-done.2
  92.8 0.0 collective-permute-done.1
  92.8 0.0 collective-permute-done
  92.8 0.0 copy-done.5
  92.8 0.9 convolution_convert_fusion
  93.7 0.0 copy-done.4
  93.8 0.7 copy.14
Async XLA Ops:
  66.4 26.5 %collective-permute-start.2 = (bf16[80,512]{1,0:T(8,128)(2,1)S(1)}, bf16[80,512]{1,0:T(8,128)(2,1)S(1)}, u32[]{:S(2)}, u32[]{:S(2)}) collective-permute-start(bf16[80,512]{1,0:T(8,128)(2,1)S(1)} %get-tuple-element.25), channel_id=1, source_target_pairs={{0,3},{1,2},{2,1},{3,0},{4,7},{5,6},{6,5},{7,4},{8,11},{9,10},{10,... | collective-permute-start | bytes 245768 | tf_op jit(solution)/shard_map/ppermute | solution.py:665
  67.6 25.2 %collective-permute-start.1 = (bf16[80,512]{1,0:T(8,128)(2,1)S(1)}, bf16[80,512]{1,0:T(8,128)(2,1)S(1)}, u32[]{:S(2)}, u32[]{:S(2)}) collective-permute-start(bf16[80,512]{1,0:T(8,128)(2,1)S(1)} %get-tuple-element.26), channel_id=1, source_target_pairs={{0,2},{1,3},{2,0},{3,1},{4,6},{5,7},{6,4},{7,5},{8,10},{9,11},{10,... | collective-permute-start | bytes 245768 | tf_op jit(solution)/shard_map/ppermute | solution.py:665
  68.6 24.3 %collective-permute-start = (bf16[80,512]{1,0:T(8,128)(2,1)S(1)}, bf16[80,512]{1,0:T(8,128)(2,1)S(1)}, u32[]{:S(2)}, u32[]{:S(2)}) collective-permute-start(bf16[80,512]{1,0:T(8,128)(2,1)S(1)} %get-tuple-element.27), channel_id=1, source_target_pairs={{0,1},{1,0},{2,3},{3,2},{4,5},{5,4},{6,7},{7,6},{8,9},{9,8},{10,11... | collective-permute-start | bytes 245768 | tf_op jit(solution)/shard_map/ppermute | solution.py:665
  70.8 2.3 %copy-start = (bf16[320,7168]{1,0:T(8,128)(2,1)S(1)}, bf16[320,7168]{1,0:T(8,128)(2,1)}, u32[]{:S(2)}) copy-start(bf16[320,7168]{1,0:T(8,128)(2,1)} %get-tuple-element.17.dy_ref) | copy-start | bytes 13762564
  73.1 2.3 %copy-start.1 = (bf16[320,7168]{1,0:T(8,128)(2,1)S(1)}, bf16[320,7168]{1,0:T(8,128)(2,1)}, u32[]{:S(2)}) copy-start(bf16[320,7168]{1,0:T(8,128)(2,1)} %get-tuple-element.18.dyr_ref) | copy-start | bytes 13762564
  75.4 1.0 %copy-start.2 = (bf16[512,320]{1,0:T(8,128)(2,1)S(1)}, bf16[512,320]{1,0:T(8,128)(2,1)}, u32[]{:S(2)}) copy-start(bf16[512,320]{1,0:T(8,128)(2,1)} %get-tuple-element.20.at_ref) | copy-start | bytes 983044
  76.4 1.0 %copy-start.3 = (bf16[512,320]{1,0:T(8,128)(2,1)S(1)}, bf16[512,320]{1,0:T(8,128)(2,1)}, u32[]{:S(2)}) copy-start(bf16[512,320]{1,0:T(8,128)(2,1)} %get-tuple-element.21.bt_ref) | copy-start | bytes 983044
  77.4 15.4 %copy-start.5 = (bf16[320,128]{1,0:T(8,128)(2,1)S(1)}, bf16[320,128]{1,0:T(8,128)(2,1)}, u32[]{:S(2)}) copy-start(bf16[320,128]{1,0:T(8,128)(2,1)} %get-tuple-element.15) | copy-start | bytes 245764
  77.4 16.3 %copy-start.4 = (bf16[128,896]{1,0:T(8,128)(2,1)S(1)}, bf16[128,896]{1,0:T(8,128)(2,1)}, u32[]{:S(2)}) copy-start(bf16[128,896]{1,0:T(8,128)(2,1)} %get-tuple-element.32) | copy-start | bytes 688132

commit v2 on v1

--- a/solution.py
+++ b/solution.py
@@ -134,7 +134,7 @@
 
 
 LANES = 128
-VMEM_LIMIT = 60 * 1024 * 1024
+VMEM_LIMIT = 40 * 1024 * 1024
 RANKS = 4
 COPIES = 80
 NT = (((1,), (1,)), ((), ()))
@@ -170,8 +170,8 @@
 
 def step_kernel(
     ids_ref, weight_ref, tok_ref, cot_ref, inw_ref, outw_ref, mean_hbm, rho_hbm, noise_hbm,
-    hid_ref, fill_ref, g_ref, at_ref, bt_ref, dy_hbm, dyr_hbm, q_hbm,
-    mean_v, delta_v, q_v, part, r_v, dy_v, rd, cs, land, xs, bs, ss, send_x,
+    hid_ref, fill_v, g0_ref, g1_ref, g2_ref, g3_ref, at_ref, bt_ref, dy_v, r_v, q_v,
+    mean_v, delta_v, part, rd, cs, land, xs, bs, ss, send_x,
     words_s, words_v, raw, up_s, up_v, h_s, h_v, one_v, plain, signed,
     send_sem, recv_sem, local_sem,
 ):
@@ -194,7 +194,7 @@
     zs = [mine, mine + 1 - 2 * (mine % 2), (mine + 2) % 4, 3 - mine]
     at_z = [(me, z) for z in zs]
     count = [0, 0]
-    started, copied = [], []
+    started = []
 
     def send(src, dst, to):
         n = count[0]
@@ -211,22 +211,20 @@
         started.append(copy)
         return copy
 
-    def local(src, dst, keep=True):
+    def local(src, dst):
         n = count[1]
         count[1] += 1
         copy = pltpu.make_async_copy(src, dst, local_sem.at[n])
         copy.start()
-        if keep:
-            copied.append(copy)
         return copy
 
     cols = [pl.ds(pl.multiple_of(owner[l] * block, LANES), block) for l in range(8)]
     got = {}
     for l in ORDER:
         got[l] = (
-            local(rho_hbm.at[:, cols[l]], delta_v.at[l], False),
-            local(noise_hbm.at[:, cols[l]], q_v.at[l], False),
-            local(mean_hbm.at[:, cols[l]], mean_v.at[l], False),
+            local(rho_hbm.at[:, cols[l]], delta_v.at[l]),
+            local(noise_hbm.at[:, cols[l]], q_v.at[l]),
+            local(mean_hbm.at[:, cols[l]], mean_v.at[l]),
         )
 
     barrier = pltpu.get_barrier_semaphore()
@@ -256,9 +254,9 @@
         two = here * jnp.where(id1 == zs[j], 1.0, 0.0)
         one_v[0, rows] = one.astype(bf16)
         one_v[1, rows] = two.astype(bf16)
-        fill_ref[rows] = (one + two).astype(bf16)
+        fill_v[rows] = (one + two).astype(bf16)
         slot_weight.append(jnp.sum(one * w0 + two * w1, axis=1, keepdims=True))
-    fill = fill_ref[...]
+    fill = fill_v[...]
     taken = dot(fill, tok_ref[...]).astype(bf16)
     xs[pl.ds(0, cap)] = taken[:cap]
     send_x[...] = taken
@@ -273,7 +271,6 @@
     raw[...] = gathered
     words_v[c, pl.ds(0, cap)] = gathered[:cap]
 
-    pl.semaphore_wait(barrier, len(peers))
     block_rows = [pl.ds(j * cap, cap) for j in range(RANKS)]
     pair_rows = [pl.ds(0, pair), pl.ds(pair, pair)]
     x_in, w_in, w_swap, up_in = {}, {}, {}, {}
@@ -287,14 +284,6 @@
     def swap_words(j):
         here = words_v.at[c, block_rows[j]]
         w_swap[j] = send(here, here, at_c)
-
-    send_rows(1)
-    send_words(1)
-    send_rows(2)
-    send_rows(3)
-    send_words(2)
-    send_words(3)
-    swap_words(0)
 
     def make_delta(l):
         got[l][0].wait()
@@ -309,8 +298,16 @@
             delta_v[l, rows] = (soft * noise).astype(bf16)
             q_v[l, rows] = (jnp.exp(rho - soft) * noise).astype(bf16)
 
-    for l in ORDER[:3]:
-        make_delta(l)
+    make_delta(ORDER[0])
+    pl.semaphore_wait(barrier, len(peers))
+    send_words(1)
+    send_rows(1)
+    send_words(2)
+    send_words(3)
+    send_rows(2)
+    send_rows(3)
+    swap_words(0)
+    make_delta(ORDER[1])
     up = dot(fill, cot_ref[...])
     for j in range(RANKS):
         mixed = (up[j * cap : (j + 1) * cap] * slot_weight[j]).astype(bf16)
@@ -320,16 +317,19 @@
             up_s[j] = mixed
     for j in range(1, RANKS):
         up_in[j] = send(up_s.at[j], up_v.at[j], at_z[j])
-    for l in ORDER[3:5]:
-        make_delta(l)
-    made = set(ORDER[:5])
+    make_delta(ORDER[2])
+    w_in[1].wait_recv()
+    swap_words(1)
+    make_delta(ORDER[3])
+    made = set(ORDER[:4])
 
     def arrive(p):
-        blocks = (1,) if p == 0 else (2, 3)
-        for j in blocks:
+        if p == 1:
+            for j in (2, 3):
+                w_in[j].wait_recv()
+                swap_words(j)
+        for j in (1,) if p == 0 else (2, 3):
             x_in[j].wait_recv()
-            w_in[j].wait_recv()
-            swap_words(j)
         rows = pair_rows[p]
         signs = signs_of(words_v[c, rows], half_words, width // LANES)
         ss[rows] = signs
@@ -368,7 +368,7 @@
 
     D_X, D_Y, N_X, N_Y, L_Y, L_X = range(6)
 
-    def reduce_first(p, middle):
+    def reduce_first(p, early, late):
         forward(p, 7)
         to_core(p, 3)
         forward(p, 6)
@@ -385,17 +385,19 @@
         forward(p, 4)
         core[p, 2].wait_recv()
         hop(p, 2, 1, N_Y, at_y)
-        middle()
+        early()
         forward(p, 1)
         to_core(p, 0)
+        reduce_last(p)
+        late()
         forward(p, 0)
+        core[p, 0].wait_recv()
 
     def reduce_last(p):
         sent[p, D_X].wait_recv()
         hop(p, 2, 0, L_Y, at_y, D_X)
         sent[p, D_Y].wait_recv()
         hop(p, 1, 1, L_X, at_x, D_Y)
-        core[p, 0].wait_recv()
 
     spread, h_in = {}, {}
 
@@ -424,15 +426,17 @@
     def gather_first(p):
         activate(p, 0)
         pass_on(p, 0, 0, 4, at_y, "y1")
-        pass_on(p, 0, 0, 2, at_x, "x2")
         pass_on(p, 0, 0, 1, at_c, "c0")
         activate(p, 1)
         pass_on(p, 1, 0, 2, at_x, "x1")
-        pass_on(p, 1, 0, 4, at_y, "y2")
         pass_on(p, 1, 0, 1, at_c, "c1")
         for j in (2 * p, 2 * p + 1):
             if j > 0:
                 h_in[j] = send(h_s.at[j], h_v.at[j], at_z[j])
+
+    def gather_second(p):
+        pass_on(p, 0, 0, 2, at_x, "x2")
+        pass_on(p, 1, 0, 4, at_y, "y2")
 
     def gather_relay(p):
         spread[p, "y1"].wait_recv()
@@ -472,24 +476,18 @@
         else:
             plain[rows] += one
             signed[rows] += two
-        if p == 1:
-            local(dy_v.at[l], dy_hbm.at[:, cols[l]])
-            local(r_v.at[l], dyr_hbm.at[:, cols[l]])
 
     arrive(0)
-    reduce_first(0, lambda: None)
-    reduce_last(0)
-    for l in range(8):
-        local(q_v.at[l], q_hbm.at[:, cols[l]])
+    reduce_first(0, lambda: None, lambda: None)
     arrive(1)
-    reduce_first(1, lambda: gather_first(0))
-    reduce_last(1)
+    reduce_first(1, lambda: gather_first(0), lambda: gather_second(0))
     at_ref[...] = xs[...].T
     bt_ref[...] = bs[...].T
     back(0, 0)
     back(0, 1, ("c0", "c1"))
     gather_relay(0)
     gather_first(1)
+    gather_second(1)
     gather_near(0)
     back(0, 2)
     back(0, 4)
@@ -521,11 +519,11 @@
     gather_last(1)
     back(1, 6)
     back(1, 7, ("c6", "c7"))
-    g_ref[...] = (plain[...] + ss[...].astype(f32) * signed[...]).astype(bf16)
+    for j, g_ref in enumerate((g0_ref, g1_ref, g2_ref, g3_ref)):
+        rows = block_rows[j]
+        g_ref[...] = (plain[rows] + ss[rows].astype(f32) * signed[rows]).astype(bf16)
     for copy in started:
         copy.wait_send()
-    for copy in copied:
-        copy.wait()
 
 
 def run_step(ids, weight, tokens, cotangent, in_words, out_words, mean, rho, noise, cap):
@@ -546,19 +544,19 @@
     return pl.pallas_call(
         step_kernel,
         in_specs=[vmem] * 6 + [hbm] * 3,
-        out_specs=[vmem] * 5 + [hbm] * 3,
+        out_specs=[vmem] * 11,
         out_shape=[
-            shape((count, block), bf16),
+            pltpu.VMEM((count, block), bf16),
             shape((slots, count), bf16),
-            shape((slots, width), bf16),
-            shape((width, slots), bf16),
-            shape((width, slots), bf16),
-            shape((slots, hidden), bf16),
-            shape((slots, hidden), bf16),
-            shape((width, hidden), bf16),
+            *[shape((cap, width), bf16)] * RANKS,
+            pltpu.VMEM((width, slots), bf16),
+            pltpu.VMEM((width, slots), bf16),
+            piece,
+            piece,
+            weights,
         ],
         scratch_shapes=[
-            weights, weights, weights, piece, piece, piece, four, four,
+            weights, weights, piece, four, four,
             pltpu.VMEM((2, 6, cap, block), bf16),
             small, small, small, small,
             pltpu.VMEM((LANES, count), jnp.int32),
@@ -582,35 +580,56 @@
     )(ids, weight, tokens, cotangent, in_words, out_words, mean, rho, noise)
 
 
-def grads_kernel(dy_ref, dyr_ref, q_ref, at_ref, bt_ref, gm_ref, gr_ref):
-    gm_ref[...] = dot(at_ref[...], dy_ref[...]).astype(gm_ref.dtype)
-    gd = dot(bt_ref[...], dyr_ref[...])
-    gr_ref[...] = (gd * q_ref[...].astype(jnp.float32)).astype(gr_ref.dtype)
-
-
-def grads(dy, dyr, q, at, bt, block):
-    slots, hidden = dy.shape
-    width = q.shape[0]
-    weight = pl.BlockSpec((width, block), lambda i: (0, i))
-    piece = pl.BlockSpec((slots, block), lambda i: (0, i))
-    whole = pl.BlockSpec((width, slots), lambda i: (0, 0))
-    out = jax.ShapeDtypeStruct((width, hidden), jnp.bfloat16)
+def grads_kernel(hid_ref, dy_ref, dyr_ref, q_ref, at_ref, bt_ref, hid_out, gm_out, gr_out, gm, gr, sem):
+    me = lax.axis_index("dp")
+    block = dy_ref.shape[2]
+    y, x, c = me // 4, (me // 2) % 2, me % 2
+    first = pltpu.make_async_copy(hid_ref, hid_out, sem.at[4])
+    first.start()
+    waiting = [None, None]
+    for l in range(8):
+        slot = l % 2
+        owner = ((y + l // 4) % 2) * 4 + ((x + (l // 2) % 2) % 2) * 2 + (c + l) % 2
+        cols = pl.ds(pl.multiple_of(owner * block, LANES), block)
+        if waiting[slot] is not None:
+            waiting[slot][0].wait()
+        gm[slot] = dot(at_ref[...], dy_ref[l]).astype(gm.dtype)
+        one = pltpu.make_async_copy(gm.at[slot], gm_out.at[:, cols], sem.at[2 * slot])
+        one.start()
+        if waiting[slot] is not None:
+            waiting[slot][1].wait()
+        gd = dot(bt_ref[...], dyr_ref[l])
+        gr[slot] = (gd * q_ref[l].astype(jnp.float32)).astype(gr.dtype)
+        two = pltpu.make_async_copy(gr.at[slot], gr_out.at[:, cols], sem.at[2 * slot + 1])
+        two.start()
+        waiting[slot] = (one, two)
+    for pair in waiting:
+        for copy in pair:
+            copy.wait()
+    first.wait()
+
+
+def grads(hid, dy, dyr, q, at, bt):
+    parts, slots, block = dy.shape
+    width = q.shape[1]
+    vmem = pl.BlockSpec(memory_space=pltpu.VMEM)
+    hbm = pl.BlockSpec(memory_space=pltpu.MemorySpace.HBM)
+    out = jax.ShapeDtypeStruct((width, parts * block), jnp.bfloat16)
+    stage = pltpu.VMEM((2, width, block), jnp.bfloat16)
     return pl.pallas_call(
         grads_kernel,
-        grid=(hidden // block,),
-        in_specs=[piece, piece, weight, whole, whole],
-        out_specs=[weight, weight],
-        out_shape=[out, out],
-        compiler_params=pltpu.CompilerParams(
-            dimension_semantics=("arbitrary",), vmem_limit_bytes=40 * 1024 * 1024
-        ),
+        in_specs=[vmem] * 6,
+        out_specs=[hbm] * 3,
+        out_shape=[jax.ShapeDtypeStruct(hid.shape, hid.dtype), out, out],
+        scratch_shapes=[stage, stage, pltpu.SemaphoreType.DMA((5,))],
+        compiler_params=pltpu.CompilerParams(vmem_limit_bytes=16 * 1024 * 1024),
         cost_estimate=pl.CostEstimate(
-            flops=4 * slots * width * hidden,
-            bytes_accessed=hidden * (6 * width + 4 * slots),
+            flops=4 * slots * width * parts * block,
+            bytes_accessed=6 * width * parts * block,
             transcendentals=0,
         ),
         name="grads",
-    )(dy, dyr, q, at, bt)
+    )(hid, dy, dyr, q, at, bt)
 
 
 def on_device(
@@ -647,7 +666,7 @@
             rho_weight,
             noise_weight,
         )
-    hidden_out, fill, g, at, bt, dy, dyr, q = run_step(
+    hidden_out, fill, g0, g1, g2, g3, at, bt, dy, dyr, q = run_step(
         expert_ids.T,
         route_weight.T,
         tokens,
@@ -659,13 +678,11 @@
         noise_weight[0],
         capacity,
     )
-    pieces = [g[:capacity]]
-    for j in range(1, ranks):
-        swap = [(z, z ^ j) for z in range(ranks)]
-        pieces.append(lax.ppermute(g[j * capacity : (j + 1) * capacity], "expert", swap))
-    grad_mean, grad_rho = grads(dy, dyr, q, at, bt, 512)
-    g_back = jnp.concatenate(pieces, axis=0)
-    grad_tokens = dot(fill, g_back, TN).astype(jnp.bfloat16)
+    pieces = [g0]
+    for j, piece in enumerate((g1, g2, g3), 1):
+        pieces.append(lax.ppermute(piece, "expert", [(z, z ^ j) for z in range(ranks)]))
+    hidden_out, grad_mean, grad_rho = grads(hidden_out, dy, dyr, q, at, bt)
+    grad_tokens = dot(fill, jnp.concatenate(pieces, axis=0), TN).astype(jnp.bfloat16)
     return (hidden_out, grad_tokens, grad_mean[None], grad_rho[None])
 
 

time: 95.1 us -> 81.3 us (0.85)
  local copies, waits for them, and re-layouts: 8.31 us -> 0.01 us
  Pallas kernels: 80.1 us -> 75.1 us
    unnamed x13 -> x4, local copies, waits for them, and re-layouts: 7.28 us -> 0.01 us
    pallas_call x1, Pallas kernels: 15.4 us -> 11.7 us  [grads(): pl.pallas_call(grads_kernel, in_specs=[vmem] * 6, out_specs=[hbm] * 3, ou...]
    pallas_call x1, Pallas kernels: 64.7 us -> 63.5 us  [run_step(): pl.pallas_call(step_kernel, in_specs=[vmem] * 6 + [hbm] * 3, out_specs=[v...]
    slice x1 -> x0, local copies, waits for them, and re-layouts: 1.03 us -> none  [on_device(): pieces = [g[:capacity]]]
  transfers between devices with their start and end apart: 3 -> 3, of which waited for: 0 -> 0; matrix products, arithmetic and copies ran while one was open for 0% -> 0% of each run, Pallas kernels for 16% -> 14%
where the time goes in v2:
time: 81.3 us; the launch traced here: 81.2 us
  Pallas kernels  75.1 us (92%)
  starting transfers between devices  4.44 us (5%)
  matrix products  0.91 us (1%)
    pallas_call x1, Pallas kernels, run_step(): pl.pallas_call(step_kernel, in_specs=[vmem] * 6 + [hbm] * 3, out_specs=[v...  63.5 us
    pallas_call x1, Pallas kernels, grads(): pl.pallas_call(grads_kernel, in_specs=[vmem] * 6, out_specs=[hbm] * 3, ou...  11.7 us
    ppermute x3, starting transfers between devices, on_device(): lax.ppermute(piece, 'expert', [(z, z ^ j) for z in range(ranks)])  4.44 us
  transfers between devices with their start and end apart: 3, of which 0 were waited for; matrix products, arithmetic and copies ran while one was open for 0% of the time, Pallas kernels for 14%

profile of v2, /device:TPU:0, one launch (start us, length us, event | category | flops | bytes accessed | tf_op | source)
XLA Modules:
  0.0 81.2 jit_solution(4530669558722527705)
XLA Ops:
  0.6 63.5 %step.1 = (bf16[128,896]{1,0:T(8,128)(2,1)S(1)}, bf16[320,128]{1,0:T(8,128)(2,1)}, bf16[80,512]{1,0:T(8,128)(2,1)}, bf16[80,512]{1,0:T(8,128)(2,1)}, bf16[80,512...) custom-call(s32[2,128]{1,0:T(2,128)} %bitcast.17, ...), custom_call_target="tpu_custom_call" | custom-call | flops 9395240960 | bytes 36700160 | tf_op jit(solution)/shard_map/step/pallas_call | solution.py:544
  64.1 0.1 collective-permute-start
  64.2 2.3 %collective-permute-start.1 = (bf16[80,512]{1,0:T(8,128)(2,1)}, bf16[80,512]{1,0:T(8,128)(2,1)S(1)}, u32[]{:S(2)}, u32[]{:S(2)}) collective-permute-start(bf16[80,512]{1,0:T(8,128)(2,1)} %get-tuple-element.28), channel_id=1, source_target_pairs={{0,2},{1,3},{2,0},{3,1},{4,6},{5,7},{6,4},{7,5},{8,10},{9,11},{10,... | collective-permute-start | bytes 245768 | tf_op jit(solution)/shard_map/ppermute | solution.py:683
  66.4 2.1 %collective-permute-start.2 = (bf16[80,512]{1,0:T(8,128)(2,1)}, bf16[80,512]{1,0:T(8,128)(2,1)S(1)}, u32[]{:S(2)}, u32[]{:S(2)}) collective-permute-start(bf16[80,512]{1,0:T(8,128)(2,1)} %get-tuple-element.29), channel_id=1, source_target_pairs={{0,3},{1,2},{2,1},{3,0},{4,7},{5,6},{6,5},{7,4},{8,11},{9,10},{10,... | collective-permute-start | bytes 245768 | tf_op jit(solution)/shard_map/ppermute | solution.py:683
  68.5 0.0 copy-start
  68.6 0.0 copy-start.1
  68.6 11.7 %grads.1 = (bf16[128,896]{1,0:T(8,128)(2,1)}, bf16[512,7168]{1,0:T(8,128)(2,1)}, bf16[512,7168]{1,0:T(8,128)(2,1)}) custom-call(bf16[128,896]{1,0:T(8,128)(2,1)S(1)} %get-tuple-element.18.hid_ref, bf16[8,320,896]{2,1,0:T(8,128)(2,1)S(1)} %get-tuple-element.19.dy_ref, bf16[8,320,896]{2,1,0:T(8,128)(2,1)S(1)} %get-tuple-element.20.dyr_ref, ...), custom_call_target="tpu_custom_call" | custom-call | flops 4697620480 | bytes 22020096 | tf_op jit(solution)/shard_map/grads/pallas_call | solution.py:619
  80.2 0.0 collective-permute-done
  80.2 0.0 collective-permute-done.1
  80.2 0.0 collective-permute-done.2
  80.3 0.0 copy-done
  80.3 0.0 copy-done.1
  80.3 0.9 %convolution_convert_fusion = bf16[128,512]{1,0:T(8,128)(2,1)} fusion(bf16[320,128]{1,0:T(8,128)(2,1)S(1)} %copy-done, bf16[80,512]{1,0:T(8,128)(2,1)S(1)} %collective-permute-done.2, bf16[80,512]{1,0:T(8,128)(2,1)S(1)} %collective-permute-done.1, bf16[80,512]{1,0:T(8,128)(2,1)S(1)} %collective-permute-done, bf16[80,512]{1,0:T(8,128)(2,1)S(1)} %copy-done.1), kind=kOutput, calls=%fused_computation | convolution fusion | flops 43319296 | bytes 540672 | tf_op jit(solution)/shard_map/dot_general | solution.py:148
Async XLA Ops:
  64.1 16.1 %collective-permute-start = (bf16[80,512]{1,0:T(8,128)(2,1)}, bf16[80,512]{1,0:T(8,128)(2,1)S(1)}, u32[]{:S(2)}, u32[]{:S(2)}) collective-permute-start(bf16[80,512]{1,0:T(8,128)(2,1)} %get-tuple-element.27), channel_id=1, source_target_pairs={{0,1},{1,0},{2,3},{3,2},{4,5},{5,4},{6,7},{7,6},{8,9},{9,8},{10,11... | collective-permute-start | bytes 245768 | tf_op jit(solution)/shard_map/ppermute | solution.py:683
  64.2 16.1 %collective-permute-start.1 = (bf16[80,512]{1,0:T(8,128)(2,1)}, bf16[80,512]{1,0:T(8,128)(2,1)S(1)}, u32[]{:S(2)}, u32[]{:S(2)}) collective-permute-start(bf16[80,512]{1,0:T(8,128)(2,1)} %get-tuple-element.28), channel_id=1, source_target_pairs={{0,2},{1,3},{2,0},{3,1},{4,6},{5,7},{6,4},{7,5},{8,10},{9,11},{10,... | collective-permute-start | bytes 245768 | tf_op jit(solution)/shard_map/ppermute | solution.py:683
  66.4 13.8 %collective-permute-start.2 = (bf16[80,512]{1,0:T(8,128)(2,1)}, bf16[80,512]{1,0:T(8,128)(2,1)S(1)}, u32[]{:S(2)}, u32[]{:S(2)}) collective-permute-start(bf16[80,512]{1,0:T(8,128)(2,1)} %get-tuple-element.29), channel_id=1, source_target_pairs={{0,3},{1,2},{2,1},{3,0},{4,7},{5,6},{6,5},{7,4},{8,11},{9,10},{10,... | collective-permute-start | bytes 245768 | tf_op jit(solution)/shard_map/ppermute | solution.py:683
  68.5 11.7 %copy-start = (bf16[320,128]{1,0:T(8,128)(2,1)S(1)}, bf16[320,128]{1,0:T(8,128)(2,1)}, u32[]{:S(2)}) copy-start(bf16[320,128]{1,0:T(8,128)(2,1)} %get-tuple-element.25) | copy-start | bytes 245764
  68.6 11.7 %copy-start.1 = (bf16[80,512]{1,0:T(8,128)(2,1)S(1)}, bf16[80,512]{1,0:T(8,128)(2,1)}, u32[]{:S(2)}) copy-start(bf16[80,512]{1,0:T(8,128)(2,1)} %get-tuple-element.26) | copy-start | bytes 245764

commit v3 on v2

--- a/solution.py
+++ b/solution.py
@@ -134,12 +134,14 @@
 
 
 LANES = 128
-VMEM_LIMIT = 40 * 1024 * 1024
+VMEM_LIMIT = 34 * 1024 * 1024
 RANKS = 4
 COPIES = 80
 NT = (((1,), (1,)), ((), ()))
 TN = (((0,), (0,)), ((), ()))
 ORDER = (7, 6, 3, 2, 5, 4, 1, 0)
+DONE = (0, 1, 2)
+LEFT = (3, 4, 5, 6, 7)
 
 
 def dot(a, b, dims=None):
@@ -170,9 +172,9 @@
 
 def step_kernel(
     ids_ref, weight_ref, tok_ref, cot_ref, inw_ref, outw_ref, mean_hbm, rho_hbm, noise_hbm,
-    hid_ref, fill_v, g0_ref, g1_ref, g2_ref, g3_ref, at_ref, bt_ref, dy_v, r_v, q_v,
-    mean_v, delta_v, part, rd, cs, land, xs, bs, ss, send_x,
-    words_s, words_v, raw, up_s, up_v, h_s, h_v, one_v, plain, signed,
+    hid_ref, fill_v, g0_ref, g1_ref, g2_ref, g3_ref, at_ref, bt_ref, dy_v, r_v, q_v, mean_v,
+    delta_v, part, rd, land, xs, bs, ss, send_x,
+    words_s, words_v, raw, up_s, up_v, h_s, h_v, one_v, plain, signed, g_s,
     send_sem, recv_sem, local_sem,
 ):
     bf16, f32 = jnp.bfloat16, jnp.float32
@@ -182,7 +184,6 @@
     width = tok_ref.shape[1]
     block = cot_ref.shape[1]
     cap = up_v.shape[1]
-    pair = 2 * cap
     slots = RANKS * cap
     in_words = inw_ref.shape[0]
     half_words = outw_ref.shape[0] // 2
@@ -272,7 +273,7 @@
     words_v[c, pl.ds(0, cap)] = gathered[:cap]
 
     block_rows = [pl.ds(j * cap, cap) for j in range(RANKS)]
-    pair_rows = [pl.ds(0, pair), pl.ds(pair, pair)]
+    span = lambda first, n: pl.ds(first * cap, n * cap)
     x_in, w_in, w_swap, up_in = {}, {}, {}, {}
 
     def send_rows(j):
@@ -289,16 +290,151 @@
         got[l][0].wait()
         got[l][1].wait()
 
-        @pl.loop(0, width // 32)
+        @pl.loop(0, width // LANES)
         def _(i):
-            rows = pl.ds(pl.multiple_of(i * 32, 32), 32)
-            rho = delta_v[l, rows].astype(f32)
+            rows = pl.ds(pl.multiple_of(i * LANES, LANES), LANES)
             noise = q_v[l, rows].astype(f32)
-            soft = jnp.log(1.0 + jnp.exp(rho))
-            delta_v[l, rows] = (soft * noise).astype(bf16)
-            q_v[l, rows] = (jnp.exp(rho - soft) * noise).astype(bf16)
-
-    make_delta(ORDER[0])
+            grown = jnp.exp(delta_v[l, rows].astype(f32))
+            more = 1.0 + grown
+            delta_v[l, rows] = (jnp.log(more) * noise).astype(bf16)
+            q_v[l, rows] = (grown / more * noise).astype(bf16)
+
+    made, loaded = set(), set()
+
+    def make(l):
+        if l not in made:
+            make_delta(l)
+            made.add(l)
+
+    def swap_in(j):
+        w_in[j].wait_recv()
+        swap_words(j)
+
+    def arrive(first, n):
+        for j in range(first, first + n):
+            if j > 0:
+                x_in[j].wait_recv()
+        rows = span(first, n)
+        signs = signs_of(words_v[c, rows], half_words, width // LANES)
+        ss[rows] = signs
+        bs[rows] = xs[rows] * signs
+        for j in range(first, first + n):
+            w_swap[j].wait_recv()
+
+    core, sent = {}, {}
+
+    def forward(first, n, l):
+        make(l)
+        if l not in loaded:
+            got[l][2].wait()
+            loaded.add(l)
+        rows = span(first, n)
+        one = dot(xs[rows], mean_v[l])
+        two = dot(bs[rows], delta_v[l])
+        signs = signs_of(
+            words_v[owner[l] // 4, rows], (owner[l] % 4) * piece_words, block // LANES
+        )
+        r_v[l, rows] = signs
+        part[l, rows] = (one + signs.astype(f32) * two).astype(bf16)
+        if l % 2:
+            core[first, l // 2] = send(part.at[l, rows], rd.at[l // 2, rows], at_c)
+
+    D, N, L = range(3)
+
+    def hop(j, k, name, to, extra=None):
+        rows = block_rows[j]
+        terms = [part[2 * k, rows], rd[k, rows]]
+        if extra is not None:
+            terms.append(land[j, extra])
+        part[2 * k, rows] = total(*terms).astype(bf16)
+        sent[j, name] = send(part.at[2 * k, rows], land.at[j, name], to)
+
+    def d_hop(j):
+        hop(j, 3, D, (at_x, at_y)[j % 2])
+
+    def n_hop(j):
+        hop(j, 1 + j % 2, N, (at_x, at_y)[j % 2])
+
+    def l_hop(j):
+        sent[j, D].wait_recv()
+        hop(j, 2 - j % 2, L, (at_y, at_x)[j % 2], D)
+
+    spread, h_in = {}, {}
+
+    def pass_on(j, l, to_l, to, name):
+        rows = block_rows[j]
+        spread[j, name] = send(dy_v.at[l, rows], dy_v.at[to_l, rows], to)
+
+    def activate(j):
+        rows = block_rows[j]
+        if j > 0:
+            up_in[j].wait_recv()
+        sent[j, N].wait_recv()
+        sent[j, L].wait_recv()
+        preact = total(part[0, rows], rd[0, rows], land[j, N], land[j, L])
+        gate = 1.0 / (1.0 + jnp.exp(-preact))
+        hidden = (preact * gate).astype(bf16)
+        slope = gate * (1.0 + preact * (1.0 - gate))
+        dy_v[0, rows] = (up_v[j].astype(f32) * slope).astype(bf16)
+        if j == 0:
+            h_v[0] = hidden
+        else:
+            h_s[j] = hidden
+
+    def g_first(j):
+        activate(j)
+        pass_on(j, 0, (4, 2)[j % 2], (at_y, at_x)[j % 2], "first")
+        pass_on(j, 0, 1, at_c, "c0")
+        if j > 0:
+            h_in[j] = send(h_s.at[j], h_v.at[j], at_z[j])
+
+    def g_second(j):
+        pass_on(j, 0, (2, 4)[j % 2], (at_x, at_y)[j % 2], "second")
+
+    def g_relay(j):
+        spread[j, "first"].wait_recv()
+        l = (4, 2)[j % 2]
+        pass_on(j, l, 6, (at_x, at_y)[j % 2], "relay")
+        pass_on(j, l, l + 1, at_c, "c%d" % l)
+
+    def g_near(j):
+        spread[j, "second"].wait_recv()
+        l = (2, 4)[j % 2]
+        pass_on(j, l, l + 1, at_c, "c%d" % l)
+
+    def g_last(j):
+        spread[j, "relay"].wait_recv()
+        pass_on(j, 6, 7, at_c, "c6")
+
+    begun = set()
+
+    def back(p, l):
+        if l % 2:
+            for j in (2 * p, 2 * p + 1):
+                spread[j, "c%d" % (l - 1)].wait_recv()
+        rows = span(2 * p, 2)
+        dy = dy_v[l, rows]
+        dyr = dy * r_v[l, rows]
+        r_v[l, rows] = dyr
+        one = dot(dy, mean_v[l], NT)
+        two = dot(dyr, delta_v[l], NT)
+        if p not in begun:
+            plain[rows] = one
+            signed[rows] = two
+            begun.add(p)
+        else:
+            plain[rows] += one
+            signed[rows] += two
+
+    def grad(l):
+        mean_v[l] = dot(at_ref[...], dy_v[l]).astype(bf16)
+        q_v[l] = (dot(bt_ref[...], r_v[l]) * q_v[l].astype(f32)).astype(bf16)
+
+    def g_make(j, ref):
+        rows = block_rows[j]
+        ref[...] = (plain[rows] + ss[rows].astype(f32) * signed[rows]).astype(bf16)
+
+    make(7)
     pl.semaphore_wait(barrier, len(peers))
     send_words(1)
     send_rows(1)
@@ -307,8 +443,30 @@
     send_rows(2)
     send_rows(3)
     swap_words(0)
-    make_delta(ORDER[1])
-    up = dot(fill, cot_ref[...])
+    make(6)
+    arrive(0, 1)
+    forward(0, 1, 7)
+    forward(0, 1, 6)
+    make(3)
+    core[0, 3].wait_recv()
+    d_hop(0)
+    swap_in(1)
+    forward(0, 1, 3)
+    forward(0, 1, 2)
+    arrive(1, 1)
+    forward(1, 1, 7)
+    core[0, 1].wait_recv()
+    n_hop(0)
+    forward(1, 1, 6)
+    make(5)
+    core[1, 3].wait_recv()
+    d_hop(1)
+    forward(0, 2, 5)
+    forward(0, 2, 4)
+    core[0, 2].wait_recv()
+    l_hop(0)
+    n_hop(1)
+    up = dot(fill_v[...], cot_ref[...])
     for j in range(RANKS):
         mixed = (up[j * cap : (j + 1) * cap] * slot_weight[j]).astype(bf16)
         if j == 0:
@@ -317,193 +475,75 @@
             up_s[j] = mixed
     for j in range(1, RANKS):
         up_in[j] = send(up_s.at[j], up_v.at[j], at_z[j])
-    make_delta(ORDER[2])
-    w_in[1].wait_recv()
-    swap_words(1)
-    make_delta(ORDER[3])
-    made = set(ORDER[:4])
-
-    def arrive(p):
-        if p == 1:
-            for j in (2, 3):
-                w_in[j].wait_recv()
-                swap_words(j)
-        for j in (1,) if p == 0 else (2, 3):
-            x_in[j].wait_recv()
-        rows = pair_rows[p]
-        signs = signs_of(words_v[c, rows], half_words, width // LANES)
-        ss[rows] = signs
-        bs[rows] = xs[rows] * signs
-        for j in (2 * p, 2 * p + 1):
-            w_swap[j].wait_recv()
-
-    def forward(p, l):
-        rows = pair_rows[p]
-        if l not in made:
-            make_delta(l)
-            made.add(l)
-        if p == 0:
-            got[l][2].wait()
-        one = dot(xs[rows], mean_v[l])
-        two = dot(bs[rows], delta_v[l])
-        signs = signs_of(
-            words_v[owner[l] // 4, rows], (owner[l] % 4) * piece_words, block // LANES
-        )
-        r_v[l, rows] = signs
-        part[l, rows] = (one + signs.astype(f32) * two).astype(bf16)
-
-    core, sent = {}, {}
-
-    def to_core(p, k):
-        rows = pair_rows[p]
-        core[p, k] = send(part.at[2 * k + 1, rows], rd.at[k, rows], at_c)
-
-    def hop(p, k, which, name, to, extra=None):
-        rows = block_rows[2 * p + which]
-        terms = [part[2 * k, rows], rd[k, rows]]
-        if extra is not None:
-            terms.append(land[p, extra])
-        cs[k, rows] = total(*terms).astype(bf16)
-        sent[p, name] = send(cs.at[k, rows], land.at[p, name], to)
-
-    D_X, D_Y, N_X, N_Y, L_Y, L_X = range(6)
-
-    def reduce_first(p, early, late):
-        forward(p, 7)
-        to_core(p, 3)
-        forward(p, 6)
-        core[p, 3].wait_recv()
-        hop(p, 3, 0, D_X, at_x)
-        hop(p, 3, 1, D_Y, at_y)
-        forward(p, 3)
-        to_core(p, 1)
-        forward(p, 2)
-        core[p, 1].wait_recv()
-        hop(p, 1, 0, N_X, at_x)
-        forward(p, 5)
-        to_core(p, 2)
-        forward(p, 4)
-        core[p, 2].wait_recv()
-        hop(p, 2, 1, N_Y, at_y)
-        early()
-        forward(p, 1)
-        to_core(p, 0)
-        reduce_last(p)
-        late()
-        forward(p, 0)
-        core[p, 0].wait_recv()
-
-    def reduce_last(p):
-        sent[p, D_X].wait_recv()
-        hop(p, 2, 0, L_Y, at_y, D_X)
-        sent[p, D_Y].wait_recv()
-        hop(p, 1, 1, L_X, at_x, D_Y)
-
-    spread, h_in = {}, {}
-
-    def pass_on(p, which, l, to_l, to, name):
-        rows = block_rows[2 * p + which]
-        spread[p, name] = send(dy_v.at[l, rows], dy_v.at[to_l, rows], to)
-
-    def activate(p, which):
-        j = 2 * p + which
-        rows = block_rows[j]
-        if j > 0:
-            up_in[j].wait_recv()
-        near, last = (N_X, L_Y) if which == 0 else (N_Y, L_X)
-        sent[p, near].wait_recv()
-        sent[p, last].wait_recv()
-        preact = total(part[0, rows], rd[0, rows], land[p, near], land[p, last])
-        gate = 1.0 / (1.0 + jnp.exp(-preact))
-        hidden = (preact * gate).astype(bf16)
-        slope = gate * (1.0 + preact * (1.0 - gate))
-        dy_v[0, rows] = (up_v[j].astype(f32) * slope).astype(bf16)
-        if j == 0:
-            h_v[0] = hidden
-        else:
-            h_s[j] = hidden
-
-    def gather_first(p):
-        activate(p, 0)
-        pass_on(p, 0, 0, 4, at_y, "y1")
-        pass_on(p, 0, 0, 1, at_c, "c0")
-        activate(p, 1)
-        pass_on(p, 1, 0, 2, at_x, "x1")
-        pass_on(p, 1, 0, 1, at_c, "c1")
-        for j in (2 * p, 2 * p + 1):
-            if j > 0:
-                h_in[j] = send(h_s.at[j], h_v.at[j], at_z[j])
-
-    def gather_second(p):
-        pass_on(p, 0, 0, 2, at_x, "x2")
-        pass_on(p, 1, 0, 4, at_y, "y2")
-
-    def gather_relay(p):
-        spread[p, "y1"].wait_recv()
-        pass_on(p, 0, 4, 6, at_x, "x3")
-        pass_on(p, 0, 4, 5, at_c, "c2")
-        spread[p, "x1"].wait_recv()
-        pass_on(p, 1, 2, 6, at_y, "y3")
-        pass_on(p, 1, 2, 3, at_c, "c3")
-
-    def gather_near(p):
-        spread[p, "x2"].wait_recv()
-        pass_on(p, 0, 2, 3, at_c, "c4")
-        spread[p, "y2"].wait_recv()
-        pass_on(p, 1, 4, 5, at_c, "c5")
-
-    def gather_last(p):
-        spread[p, "x3"].wait_recv()
-        pass_on(p, 0, 6, 7, at_c, "c6")
-        spread[p, "y3"].wait_recv()
-        pass_on(p, 1, 6, 7, at_c, "c7")
-
-    first_back = {0: True, 1: True}
-
-    def back(p, l, waits=()):
-        for name in waits:
-            spread[p, name].wait_recv()
-        rows = pair_rows[p]
-        dy = dy_v[l, rows]
-        dyr = dy * r_v[l, rows]
-        r_v[l, rows] = dyr
-        one = dot(dy, mean_v[l], NT)
-        two = dot(dyr, delta_v[l], NT)
-        if first_back[p]:
-            plain[rows] = one
-            signed[rows] = two
-            first_back[p] = False
-        else:
-            plain[rows] += one
-            signed[rows] += two
-
-    arrive(0)
-    reduce_first(0, lambda: None, lambda: None)
-    arrive(1)
-    reduce_first(1, lambda: gather_first(0), lambda: gather_second(0))
+    forward(1, 1, 3)
+    forward(1, 1, 2)
+    make(1)
+    core[1, 1].wait_recv()
+    l_hop(1)
+    swap_in(2)
+    swap_in(3)
+    forward(0, 2, 1)
+    forward(0, 2, 0)
+    core[0, 0].wait_recv()
+    g_first(0)
+    g_second(0)
+    arrive(2, 2)
+    forward(2, 2, 7)
+    forward(2, 2, 6)
+    core[2, 3].wait_recv()
+    d_hop(2)
+    d_hop(3)
+    forward(2, 2, 3)
+    forward(2, 2, 2)
+    g_first(1)
+    core[2, 1].wait_recv()
+    n_hop(2)
+    forward(2, 2, 5)
+    forward(2, 2, 4)
+    core[2, 2].wait_recv()
+    n_hop(3)
+    forward(2, 2, 1)
+    l_hop(2)
+    l_hop(3)
+    g_relay(0)
+    g_second(1)
+    forward(2, 2, 0)
     at_ref[...] = xs[...].T
     bt_ref[...] = bs[...].T
-    back(0, 0)
-    back(0, 1, ("c0", "c1"))
-    gather_relay(0)
-    gather_first(1)
-    gather_second(1)
-    gather_near(0)
-    back(0, 2)
+    g_relay(1)
+    g_near(0)
+    for l in (0, 1, 2, 3):
+        back(0, l)
+    core[2, 0].wait_recv()
+    g_first(2)
+    g_first(3)
+    g_second(2)
+    g_second(3)
+    back(1, 0)
+    g_near(1)
     back(0, 4)
-    back(0, 3, ("c3", "c4"))
-    back(0, 5, ("c2", "c5"))
-    back(1, 0)
-    back(1, 1, ("c0", "c1"))
-    gather_last(0)
+    back(0, 5)
+    g_last(0)
+    back(1, 1)
+    g_last(1)
+    grad(0)
     back(0, 6)
-    back(0, 7, ("c6", "c7"))
-    gather_relay(1)
-    gather_near(1)
+    back(0, 7)
+    g_make(0, g0_ref)
+    g_make(1, g_s)
+    g_in = send(g_s, g1_ref, at_z[1])
+    g_relay(3)
+    g_relay(2)
+    grad(1)
+    g_near(2)
     back(1, 2)
+    g_near(3)
     back(1, 4)
-    back(1, 3, ("c3", "c4"))
-    back(1, 5, ("c2", "c5"))
+    grad(2)
+    back(1, 3)
+    g_last(2)
+    g_last(3)
+    back(1, 5)
     for j in range(1, RANKS):
         h_in[j].wait_recv()
     out = None
@@ -516,12 +556,11 @@
         picked = picked * column
         out = picked if out is None else out + picked
     hid_ref[...] = out.astype(bf16)
-    gather_last(1)
     back(1, 6)
-    back(1, 7, ("c6", "c7"))
-    for j, g_ref in enumerate((g0_ref, g1_ref, g2_ref, g3_ref)):
-        rows = block_rows[j]
-        g_ref[...] = (plain[rows] + ss[rows].astype(f32) * signed[rows]).astype(bf16)
+    back(1, 7)
+    g_make(2, g2_ref)
+    g_make(3, g3_ref)
+    g_in.wait_recv()
     for copy in started:
         copy.wait_send()
 
@@ -544,20 +583,21 @@
     return pl.pallas_call(
         step_kernel,
         in_specs=[vmem] * 6 + [hbm] * 3,
-        out_specs=[vmem] * 11,
+        out_specs=[vmem] * 12,
         out_shape=[
             pltpu.VMEM((count, block), bf16),
-            shape((slots, count), bf16),
-            *[shape((cap, width), bf16)] * RANKS,
+            pltpu.VMEM((slots, count), bf16),
+            *[pltpu.VMEM((cap, width), bf16)] * RANKS,
             pltpu.VMEM((width, slots), bf16),
             pltpu.VMEM((width, slots), bf16),
             piece,
             piece,
             weights,
+            weights,
         ],
         scratch_shapes=[
-            weights, weights, piece, four, four,
-            pltpu.VMEM((2, 6, cap, block), bf16),
+            weights, piece, four,
+            pltpu.VMEM((RANKS, 3, cap, block), bf16),
             small, small, small, small,
             pltpu.VMEM((LANES, count), jnp.int32),
             pltpu.VMEM((2, slots, LANES), jnp.int32),
@@ -566,6 +606,7 @@
             pltpu.VMEM((2, slots, count), bf16),
             pltpu.VMEM((slots, width), f32),
             pltpu.VMEM((slots, width), f32),
+            pltpu.VMEM((cap, width), bf16),
             pltpu.SemaphoreType.DMA((COPIES,)),
             pltpu.SemaphoreType.DMA((COPIES,)),
             pltpu.SemaphoreType.DMA((COPIES,)),
@@ -580,56 +621,56 @@
     )(ids, weight, tokens, cotangent, in_words, out_words, mean, rho, noise)
 
 
-def grads_kernel(hid_ref, dy_ref, dyr_ref, q_ref, at_ref, bt_ref, hid_out, gm_out, gr_out, gm, gr, sem):
+def grads_kernel(
+    hid_ref, dy_ref, dyr_ref, q_ref, mean_ref, at_ref, bt_ref, hid_out, gm_out, gr_out, gm, gr, sem
+):
     me = lax.axis_index("dp")
     block = dy_ref.shape[2]
     y, x, c = me // 4, (me // 2) % 2, me % 2
-    first = pltpu.make_async_copy(hid_ref, hid_out, sem.at[4])
-    first.start()
-    waiting = [None, None]
-    for l in range(8):
-        slot = l % 2
+    copies = [pltpu.make_async_copy(hid_ref, hid_out, sem.at[16])]
+    copies[0].start()
+
+    def store(src, out, l, n):
         owner = ((y + l // 4) % 2) * 4 + ((x + (l // 2) % 2) % 2) * 2 + (c + l) % 2
         cols = pl.ds(pl.multiple_of(owner * block, LANES), block)
-        if waiting[slot] is not None:
-            waiting[slot][0].wait()
-        gm[slot] = dot(at_ref[...], dy_ref[l]).astype(gm.dtype)
-        one = pltpu.make_async_copy(gm.at[slot], gm_out.at[:, cols], sem.at[2 * slot])
-        one.start()
-        if waiting[slot] is not None:
-            waiting[slot][1].wait()
+        copy = pltpu.make_async_copy(src, out.at[:, cols], sem.at[n])
+        copy.start()
+        copies.append(copy)
+
+    for l in DONE:
+        store(mean_ref.at[l], gm_out, l, 2 * l)
+        store(q_ref.at[l], gr_out, l, 2 * l + 1)
+    for i, l in enumerate(LEFT):
+        gm[i] = dot(at_ref[...], dy_ref[l]).astype(gm.dtype)
+        store(gm.at[i], gm_out, l, 2 * l)
         gd = dot(bt_ref[...], dyr_ref[l])
-        gr[slot] = (gd * q_ref[l].astype(jnp.float32)).astype(gr.dtype)
-        two = pltpu.make_async_copy(gr.at[slot], gr_out.at[:, cols], sem.at[2 * slot + 1])
-        two.start()
-        waiting[slot] = (one, two)
-    for pair in waiting:
-        for copy in pair:
-            copy.wait()
-    first.wait()
-
-
-def grads(hid, dy, dyr, q, at, bt):
+        gr[i] = (gd * q_ref[l].astype(jnp.float32)).astype(gr.dtype)
+        store(gr.at[i], gr_out, l, 2 * l + 1)
+    for copy in copies:
+        copy.wait()
+
+
+def grads(hid, dy, dyr, q, mean, at, bt):
     parts, slots, block = dy.shape
     width = q.shape[1]
     vmem = pl.BlockSpec(memory_space=pltpu.VMEM)
     hbm = pl.BlockSpec(memory_space=pltpu.MemorySpace.HBM)
     out = jax.ShapeDtypeStruct((width, parts * block), jnp.bfloat16)
-    stage = pltpu.VMEM((2, width, block), jnp.bfloat16)
+    stage = pltpu.VMEM((len(LEFT), width, block), jnp.bfloat16)
     return pl.pallas_call(
         grads_kernel,
-        in_specs=[vmem] * 6,
+        in_specs=[vmem] * 7,
         out_specs=[hbm] * 3,
         out_shape=[jax.ShapeDtypeStruct(hid.shape, hid.dtype), out, out],
-        scratch_shapes=[stage, stage, pltpu.SemaphoreType.DMA((5,))],
-        compiler_params=pltpu.CompilerParams(vmem_limit_bytes=16 * 1024 * 1024),
+        scratch_shapes=[stage, stage, pltpu.SemaphoreType.DMA((17,))],
+        compiler_params=pltpu.CompilerParams(vmem_limit_bytes=20 * 1024 * 1024),
         cost_estimate=pl.CostEstimate(
             flops=4 * slots * width * parts * block,
             bytes_accessed=6 * width * parts * block,
             transcendentals=0,
         ),
         name="grads",
-    )(hid, dy, dyr, q, at, bt)
+    )(hid, dy, dyr, q, mean, at, bt)
 
 
 def on_device(
@@ -666,7 +707,7 @@
             rho_weight,
             noise_weight,
         )
-    hidden_out, fill, g0, g1, g2, g3, at, bt, dy, dyr, q = run_step(
+    hidden_out, fill, g0, g1, g2, g3, at, bt, dy, dyr, q, mean = run_step(
         expert_ids.T,
         route_weight.T,
         tokens,
@@ -678,10 +719,10 @@
         noise_weight[0],
         capacity,
     )
-    pieces = [g0]
-    for j, piece in enumerate((g1, g2, g3), 1):
+    pieces = [g0, g1]
+    for j, piece in ((2, g2), (3, g3)):
         pieces.append(lax.ppermute(piece, "expert", [(z, z ^ j) for z in range(ranks)]))
-    hidden_out, grad_mean, grad_rho = grads(hidden_out, dy, dyr, q, at, bt)
+    hidden_out, grad_mean, grad_rho = grads(hidden_out, dy, dyr, q, mean, at, bt)
     grad_tokens = dot(fill, jnp.concatenate(pieces, axis=0), TN).astype(jnp.bfloat16)
     return (hidden_out, grad_tokens, grad_mean[None], grad_rho[None])
 

time: 81.3 us -> 69.3 us (0.85)
  Pallas kernels: 75.1 us -> 64.9 us
  starting transfers between devices: 4.44 us -> 2.62 us
    pallas_call x1, Pallas kernels: 11.7 us -> 6.35 us  [grads(): pl.pallas_call(grads_kernel, in_specs=[vmem] * 7, out_specs=[hbm] * 3, ou...]
    pallas_call x1, Pallas kernels: 63.5 us -> 58.6 us  [run_step(): pl.pallas_call(step_kernel, in_specs=[vmem] * 6 + [hbm] * 3, out_specs=[v...]
    ppermute x3 -> x2, starting transfers between devices: 4.44 us -> 2.62 us  [on_device(): lax.ppermute(piece, 'expert', [(z, z ^ j) for z in range(ranks)])]
  transfers between devices with their start and end apart: 3 -> 2, of which waited for: 0 -> 0; matrix products, arithmetic and copies ran while one was open for 0% -> 0% of each run, Pallas kernels for 14% -> 9%
where the time goes in v3:
time: 69.3 us; the launch traced here: 69.1 us
  Pallas kernels  64.9 us (94%)
  starting transfers between devices  2.62 us (4%)
  matrix products  0.91 us (1%)
    pallas_call x1, Pallas kernels, run_step(): pl.pallas_call(step_kernel, in_specs=[vmem] * 6 + [hbm] * 3, out_specs=[v...  58.6 us
    pallas_call x1, Pallas kernels, grads(): pl.pallas_call(grads_kernel, in_specs=[vmem] * 7, out_specs=[hbm] * 3, ou...  6.35 us
    ppermute x2, starting transfers between devices, on_device(): lax.ppermute(piece, 'expert', [(z, z ^ j) for z in range(ranks)])  2.62 us
  transfers between devices with their start and end apart: 2, of which 0 were waited for; matrix products, arithmetic and copies ran while one was open for 0% of the time, Pallas kernels for 9%

profile of v3, /device:TPU:0, one launch (start us, length us, event | category | flops | bytes accessed | tf_op | source)
XLA Modules:
  0.0 69.1 jit_solution(5849107950427541456)
XLA Ops:
  0.6 58.6 %step.1 = (bf16[128,896]{1,0:T(8,128)(2,1)S(1)}, bf16[320,128]{1,0:T(8,128)(2,1)S(1)}, bf16[80,512]{1,0:T(8,128)(2,1)S(1)}, bf16[80,512]{1,0:T(8,128)(2,1)S(1)},...) custom-call(s32[2,128]{1,0:T(2,128)} %bitcast.17, ...), custom_call_target="tpu_custom_call" | custom-call | flops 9395240960 | bytes 36700160 | tf_op jit(solution)/shard_map/step/pallas_call | solution.py:583
  59.2 1.0 %collective-permute-start = (bf16[80,512]{1,0:T(8,128)(2,1)S(1)}, bf16[80,512]{1,0:T(8,128)(2,1)S(1)}, u32[]{:S(2)}, u32[]{:S(2)}) collective-permute-start(bf16[80,512]{1,0:T(8,128)(2,1)S(1)} %get-tuple-element.30), channel_id=1, source_target_pairs={{0,2},{1,3},{2,0},{3,1},{4,6},{5,7},{6,4},{7,5},{8,10},{9,11},{10,... | collective-permute-start | bytes 245768 | tf_op jit(solution)/shard_map/ppermute | solution.py:724
  60.3 1.6 %collective-permute-start.1 = (bf16[80,512]{1,0:T(8,128)(2,1)S(1)}, bf16[80,512]{1,0:T(8,128)(2,1)S(1)}, u32[]{:S(2)}, u32[]{:S(2)}) collective-permute-start(bf16[80,512]{1,0:T(8,128)(2,1)S(1)} %get-tuple-element.31), channel_id=1, source_target_pairs={{0,3},{1,2},{2,1},{3,0},{4,7},{5,6},{6,5},{7,4},{8,11},{9,10},{10,... | collective-permute-start | bytes 245768 | tf_op jit(solution)/shard_map/ppermute | solution.py:724
  61.9 6.3 %grads.1 = (bf16[128,896]{1,0:T(8,128)(2,1)}, bf16[512,7168]{1,0:T(8,128)(2,1)}, bf16[512,7168]{1,0:T(8,128)(2,1)}) custom-call(bf16[128,896]{1,0:T(8,128)(2,1)S(1)} %get-tuple-element.19.hid_ref, bf16[8,320,896]{2,1,0:T(8,128)(2,1)S(1)} %get-tuple-element.20.dy_ref, bf16[8,320,896]{2,1,0:T(8,128)(2,1)S(1)} %get-tuple-element.21.dyr_ref, ...), custom_call_target="tpu_custom_call" | custom-call | flops 4697620480 | bytes 22020096 | tf_op jit(solution)/shard_map/grads/pallas_call | solution.py:660
  68.2 0.0 collective-permute-done
  68.2 0.0 collective-permute-done.1
  68.2 0.9 %convolution_convert_fusion = bf16[128,512]{1,0:T(8,128)(2,1)} fusion(bf16[320,128]{1,0:T(8,128)(2,1)S(1)} %get-tuple-element.27, bf16[80,512]{1,0:T(8,128)(2,1)S(1)} %collective-permute-done.1, bf16[80,512]{1,0:T(8,128)(2,1)S(1)} %collective-permute-done, bf16[80,512]{1,0:T(8,128)(2,1)S(1)} %get-tuple-element.29, bf16[80,512]{1,0:T(8,128)(2,1)S(1)} %get-tuple-element.28), kind=kOutput, calls=%fused_computation | convolution fusion | flops 43319296 | bytes 540672 | tf_op jit(solution)/shard_map/dot_general | solution.py:150
Async XLA Ops:
  59.2 9.0 %collective-permute-start = (bf16[80,512]{1,0:T(8,128)(2,1)S(1)}, bf16[80,512]{1,0:T(8,128)(2,1)S(1)}, u32[]{:S(2)}, u32[]{:S(2)}) collective-permute-start(bf16[80,512]{1,0:T(8,128)(2,1)S(1)} %get-tuple-element.30), channel_id=1, source_target_pairs={{0,2},{1,3},{2,0},{3,1},{4,6},{5,7},{6,4},{7,5},{8,10},{9,11},{10,... | collective-permute-start | bytes 245768 | tf_op jit(solution)/shard_map/ppermute | solution.py:724
  60.3 8.0 %collective-permute-start.1 = (bf16[80,512]{1,0:T(8,128)(2,1)S(1)}, bf16[80,512]{1,0:T(8,128)(2,1)S(1)}, u32[]{:S(2)}, u32[]{:S(2)}) collective-permute-start(bf16[80,512]{1,0:T(8,128)(2,1)S(1)} %get-tuple-element.31), channel_id=1, source_target_pairs={{0,3},{1,2},{2,1},{3,0},{4,7},{5,6},{6,5},{7,4},{8,11},{9,10},{10,... | collective-permute-start | bytes 245768 | tf_op jit(solution)/shard_map/ppermute | solution.py:724
